TPU v7x, 32 devices: a whole 2x2x4 slice. The times are simulated.
32 devices in a mesh: gz: 8 (over z, y), gy: 4 (over x, core).
Axes of the slice: x: 2, y: 2, z: 4, core: 2. Of those that a mesh axis runs over, the one named last changes fastest.
Arguments:
- charges: float32 [64, 64, 1024], P('gz', 'gy'), may hold values from -6 to 6
- kernel: float32 [64, 64, 64], P('gz', 'gy'), may hold values from -0.01171875 to 0.01171875
Outputs:
- fine_potential: float32 [128, 128, 2048], P('gz', 'gy')
All inputs are finite; a program needn't handle non-finite values.
Results may differ from a plain program's by a relative error of at most 0.000098.
Values sent between devices are 32-bit elements; how exact they have to be, the bound alone decides.
No kernel may reach another device: no remote copies, remote signals or barrier semaphores. Data moves between devices by JAX's collectives and lax.ppermute only.
A program may use at most 128 MiB of HBM per device.

v0:
```python
import functools
import math

import jax
import jax.numpy as jnp
import numpy as np
from jax import lax
from jax.experimental import pallas as pl
from jax.experimental.pallas import tpu as pltpu
from jax.sharding import PartitionSpec as P

LANES = 128
SUBLANES = 8
TAPS = ((-1, -1.0 / 16.0), (0, 9.0 / 16.0), (1, 9.0 / 16.0), (2, -1.0 / 16.0))
VMEM = pl.BlockSpec(memory_space=pltpu.VMEM)
NT = (((1,), (1,)), ((), ()))
NN = (((1,), (0,)), ((), ()))


class Plan:
    def __init__(self, planes, rows, count, replicas, nz, ny):
        self.planes, self.rows, self.count, self.replicas = planes, rows, count, replicas
        self.nz, self.ny = nz, ny
        self.fine_x = LANES // replicas
        self.radix = count // self.fine_x
        self.parts = nz * ny
        self.block = 2 * replicas
        self.sent = self.block + 2
        self.back = self.block + 3 * self.block // 4
        half = self.radix // 2
        groups = [(0, list(range(0, count // 2, self.radix)))]
        groups.append((half, list(range(half, count // 2, self.radix))))
        for first in range(1, half):
            groups.append((first, list(range(first, count, self.radix))))
        self.groups = groups

    @staticmethod
    def fits(planes, rows, count, replicas, nz, ny):
        if planes * rows != LANES or rows % SUBLANES or 2 * rows * 4 != LANES:
            return False
        if LANES % replicas or replicas % SUBLANES or 2 * replicas != 4 * SUBLANES:
            return False
        fine_x = LANES // replicas
        if count % (2 * fine_x):
            return False
        powers = (count // fine_x, nz, ny, fine_x)
        if any(size & (size - 1) for size in powers):
            return False
        return nz * ny * 2 == count and nz > 2 and ny > 2 and count // fine_x >= 4


def halves(table):
    high = np.asarray(table, np.float32).astype(jnp.bfloat16)
    low = (np.asarray(table, np.float64) - high.astype(np.float64)).astype(jnp.bfloat16)
    return high, low


def side_by_side(table):
    return np.concatenate(halves(table), axis=1)


def spread(small, replicas):
    return np.kron(small, np.eye(replicas))


def slot_rows(plan, modes, at):
    made = []
    for mode in modes:
        angle = 2.0 * np.pi * mode * at / plan.count
        if mode == 0:
            made.append(np.concatenate([np.cos(angle), np.sin(angle)]))
            flip = np.pi * at
            made.append(np.concatenate([np.cos(flip), np.sin(flip)]))
        else:
            made.append(np.concatenate([np.cos(angle), np.sin(angle)]))
            made.append(np.concatenate([-np.sin(angle), np.cos(angle)]))
    return np.stack(made)


def pack_tables(plan):
    at = np.arange(plan.fine_x)
    real, full = [], []
    for first, modes in plan.groups:
        small = slot_rows(plan, modes, at)
        if first in (0, plan.radix // 2):
            real.append(side_by_side(spread(small[:, : plan.fine_x], plan.replicas)))
        else:
            full.append(side_by_side(spread(small, plan.replicas)))
    modes = [mode for _, group in plan.groups for mode in group]
    every = slot_rows(plan, modes, np.arange(plan.count))[:, : plan.count]
    every = np.concatenate([every[0::2], every[1::2]])
    return np.concatenate(real), np.concatenate(full), every.astype(np.float32)


def unpack_tables(plan):
    at = np.arange(plan.fine_x)
    real, full = [], []
    for first, modes in plan.groups:
        rows = slot_rows(plan, modes, at)
        re_of, im_of = rows[:, : plan.fine_x].T, rows[:, plan.fine_x :].T
        if first in (0, plan.radix // 2):
            weight = np.full(re_of.shape, 2.0 / plan.count)
            if first == 0:
                weight[:, :2] = 1.0 / plan.count
            real.append(side_by_side(spread(re_of * weight, plan.replicas)))
        else:
            both = np.concatenate([re_of, im_of]) / plan.count
            full.append(side_by_side(spread(both, plan.replicas)))
    return np.concatenate(real), np.concatenate(full)


def plane_tables(plan):
    count = plan.count
    z_at = np.repeat(np.arange(plan.planes), plan.rows)
    y_at = np.tile(np.arange(plan.rows), plan.planes)
    z_of = np.repeat(np.arange(plan.nz), plan.ny)
    y_of = np.tile(np.arange(plan.ny), plan.nz)
    angle = 2 * np.pi * (np.outer(z_of, z_at) + np.outer(y_of, y_at)) / count
    twist = np.concatenate([np.cos(angle), -np.sin(angle)]).astype(np.float32)
    angle = 2 * np.pi * (np.outer(z_at, z_at) / plan.planes + np.outer(y_at, y_at) / plan.rows)
    cosine, sine = np.cos(angle), np.sin(angle)
    there = np.block([[cosine, -sine], [sine, cosine]])
    scale = 1.0 / (count * count)
    again = np.block([[cosine, sine], [-sine, cosine]]) * scale
    angle = 2 * np.pi * (np.outer(z_of, z_of) / plan.nz + np.outer(y_of, y_of) / plan.ny)
    cosine, sine = np.cos(angle), np.sin(angle)
    blocks = np.block([[cosine, sine], [-sine, cosine], [cosine, -sine], [-sine, -cosine]])
    return twist, side_by_side(there), side_by_side(again), blocks.astype(np.float32)


def halo_moves(plan):
    planes, rows = plan.planes, plan.rows
    quarter = LANES // 4
    taken = {0, 1, planes - 1}
    open_groups = [
        g for g in range(planes)
        if g not in taken and not 2 * quarter <= g * rows < 3 * quarter
    ]
    used = {g: 0 for g in open_groups}
    moves, where = [], {}
    for source, left in (("own", set(range(planes))), ("corner", {planes - 1, 0, 1})):
        while left:
            best = None
            for shift in range(planes):
                for slot in range(rows // 3):
                    hits = [
                        z for z in left
                        if (z + shift) % planes in used and used[(z + shift) % planes] == slot
                    ]
                    if best is None or len(hits) > len(best[2]):
                        best = (shift, slot, hits)
            shift, slot, hits = best
            lanes = []
            for z in hits:
                group = (z + shift) % planes
                used[group] += 1
                left.discard(z)
                plane = z
                if source == "corner":
                    plane = -1 if z == planes - 1 else planes + z
                for step, row in enumerate((rows, rows + 1, -1)):
                    lane = group * rows + 3 * slot + step
                    lanes.append(lane)
                    where[(plane, row)] = lane
            moves.append((source, (shift * rows + 3 * slot) % LANES, tuple(sorted(lanes))))
    for row in range(rows):
        where[(-1, row)] = (planes - 1) * rows + row
        where[(planes, row)] = row
        where[(planes + 1, row)] = rows + row
    return moves, where


def stencil_table(plan):
    _, where = halo_moves(plan)

    def line(size):
        made = np.zeros((2 * size, size + 3))
        for i in range(size):
            made[2 * i, i + 1] = 1.0
            for step, weight in TAPS:
                made[2 * i + 1, i + 1 + step] = weight
        return made

    along_z, along_y = line(plan.planes), line(plan.rows)
    table = np.zeros((4 * plan.planes * plan.rows, 2 * LANES))
    for z in range(-1, plan.planes + 2):
        for y in range(-1, plan.rows + 2):
            if 0 <= z < plan.planes and 0 <= y < plan.rows:
                lane = z * plan.rows + y
            else:
                lane = LANES + where[(z, y)]
            table[:, lane] = np.kron(along_z[:, z + 1], along_y[:, y + 1])
    return table.astype(jnp.bfloat16)


def split(values):
    high = values.astype(jnp.bfloat16)
    low = (values - high.astype(jnp.float32)).astype(jnp.bfloat16)
    return high, low


def dot(a, b, dims):
    return lax.dot_general(a, b, dims, preferred_element_type=jnp.float32)


def dot_exact(a, b, dims):
    return lax.dot_general(
        a, b, dims, precision=lax.Precision.HIGHEST, preferred_element_type=jnp.float32
    )


def add(a, b):
    if a is None:
        return b
    return a if b is None else a + b


def sub(a, b):
    if b is None:
        return a
    return -b if a is None else a - b


def turn(value, angle):
    re, im = value
    c, s = math.cos(angle), math.sin(angle)
    near = 1e-9
    if abs(s) < near:
        return value if c > 0 else (sub(None, re) if re is not None else None, sub(None, im) if im is not None else None)
    if abs(c) < near:
        minus = lambda v: None if v is None else -v
        return (minus(im), re) if s > 0 else (im, minus(re))
    if abs(abs(c) - abs(s)) < near:
        c_sign, s_sign = math.copysign(1.0, c), math.copysign(1.0, s)
        size = abs(c)
        if im is None:
            scaled = re * size
            return (scaled if c_sign > 0 else -scaled, scaled if s_sign > 0 else -scaled)
        first = (re - im) if c_sign * s_sign > 0 else (re + im)
        second = (re + im) if c_sign * s_sign > 0 else (im - re)
        return (first * (c_sign * size), second * (c_sign * size))
    if im is None:
        return (re * c, re * s)
    return (re * c - im * s, re * s + im * c)


def transform(values, sign):
    size = len(values)
    if size == 1:
        return values
    even, odd = transform(values[0::2], sign), transform(values[1::2], sign)
    first, second = [], []
    for k in range(size // 2):
        e, o = even[k], turn(odd[k], sign * 2.0 * math.pi * k / size)
        first.append((add(e[0], o[0]), add(e[1], o[1])))
        second.append((sub(e[0], o[0]), sub(e[1], o[1])))
    return first + second


def from_real(values):
    size = len(values)
    if size == 2:
        return [(values[0] + values[1], None), (values[0] - values[1], None)]
    even, odd = from_real(values[0::2]), from_real(values[1::2])
    made = [None] * (size // 2 + 1)
    for k in range(size // 4 + 1):
        e, o = even[k], turn(odd[k], -2.0 * math.pi * k / size)
        made[k] = (add(e[0], o[0]), add(e[1], o[1]))
        if size // 2 - k != k:
            other = (sub(e[0], o[0]), sub(e[1], o[1]))
            made[size // 2 - k] = (other[0], None if other[1] is None else -other[1])
    made[0] = (made[0][0], None)
    made[size // 2] = (made[size // 2][0], None)
    return made


def to_real(values):
    half = len(values) - 1
    size = 2 * half
    if size == 2:
        a, b = values[0][0], values[1][0]
        return [a + b, a - b]
    even, odd = [], []
    for k in range(half // 2 + 1):
        a = values[k]
        b = values[half - k]
        b = (b[0], None if b[1] is None else -b[1])
        if k == half // 2:
            even.append((a[0] + b[0], None))
            odd.append((turn((None, sub(a[1], b[1])), 2.0 * math.pi * k / size)[0], None))
            continue
        even.append((add(a[0], b[0]), add(a[1], b[1])))
        odd.append(turn((sub(a[0], b[0]), sub(a[1], b[1])), 2.0 * math.pi * k / size))
    made = [None] * size
    made[0::2] = to_real(even)
    made[1::2] = to_real(odd)
    return made


def pack_kernel(plan, charges, kernel, real_table, full_table, kernel_table, out):
    width, block = LANES, plan.block
    tiles = [
        charges[:, :, a * width : (a + 1) * width].reshape(LANES, width)
        for a in range(plan.radix)
    ]
    spectrum = from_real(tiles)
    slot, real_at, full_at = 0, 0, 0
    for first, modes in plan.groups:
        re, im = spectrum[first]
        size = len(modes) * block
        if im is None:
            columns, table, at = width, real_table, real_at
            real_at += size
            values = re
        else:
            columns, table, at = 2 * width, full_table, full_at
            full_at += size
            values = jnp.concatenate([re, im], axis=1)
        high, low = split(values)
        w_high = table[at : at + size, :columns]
        w_low = table[at : at + size, columns:]
        made = dot(
            jnp.concatenate([w_high, w_high, w_low], axis=1),
            jnp.concatenate([high, low, high], axis=1),
            NT,
        )
        for m in range(len(modes)):
            start = (slot + m) * plan.sent
            out[start : start + block, :] = made[m * block : (m + 1) * block]
        slot += len(modes)
    made = dot_exact(kernel_table[...], kernel[...].reshape(LANES, plan.count), NT)
    for c in range(2):
        rows = pl.ds(block + c, plan.parts, stride=plan.sent)
        out[rows, :] = made[c * plan.parts : (c + 1) * plan.parts]


def plane_kernel(
    plan, shared, arrived, twist, there, again, blocks, out,
    first_pass, spectra, gains, high_part, low_part,
):
    nz, ny, parts, reps = plan.nz, plan.ny, plan.parts, plan.replicas
    whole = 2 * LANES

    def both(table):
        high, low = table[:, :whole], table[:, whole:]
        return jnp.concatenate([high, high, low], axis=0)

    def apply(table, size):
        high, low = high_part[:size, :], low_part[:size, :]
        return dot(jnp.concatenate([high, low, high], axis=1), both(table), NN)

    def twisted(re, im, t, sign):
        c = twist[t : t + 1, :]
        s = twist[parts + t : parts + t + 1, :] * sign
        return re * c - im * s, re * s + im * c

    def put(at, size, re, im):
        high, low = split(jnp.concatenate([re, im], axis=1))
        high_part[at : at + size, :] = high
        low_part[at : at + size, :] = low

    lines = jnp.concatenate(
        [arrived[pl.ds(plan.block + c, parts, stride=plan.sent), :] for c in range(2)]
    )
    lines = dot_exact(blocks[...], lines, NN)
    c, s = twist[:parts, :], twist[parts:, :]
    for k in range(2):
        re = lines[2 * k * parts : (2 * k + 1) * parts]
        im = lines[(2 * k + 1) * parts : (2 * k + 2) * parts]
        put(k * parts, parts, re * c - im * s, re * s + im * c)
    made = apply(there, 2 * parts)
    plus_re, plus_im = made[:parts, :LANES], made[:parts, LANES:]
    minus_re, minus_im = made[parts:, :LANES], made[parts:, LANES:]
    a_re, a_im = 0.5 * (plus_re + minus_re), 0.5 * (plus_im + minus_im)
    b_re, b_im = 0.5 * (plus_im - minus_im), 0.5 * (minus_re - plus_re)
    is_shared = shared[0] == 0
    zero = jnp.zeros_like(a_re)
    gains[0 * parts : 1 * parts, :] = jnp.where(is_shared, 0.5 * (a_re + b_re), plus_re)
    gains[1 * parts : 2 * parts, :] = jnp.where(is_shared, 0.5 * (a_im + b_im), plus_im)
    gains[2 * parts : 3 * parts, :] = jnp.where(is_shared, 0.5 * (a_re - b_re), zero)
    gains[3 * parts : 4 * parts, :] = jnp.where(is_shared, 0.5 * (a_im - b_im), zero)

    for gy in range(ny):
        values = []
        for gz in range(nz):
            at = (gz * ny + gy) * plan.sent
            values.append((arrived[at : at + reps, :], arrived[at + reps : at + 2 * reps, :]))
        for kz, (re, im) in enumerate(transform(values, -1)):
            at = (kz * ny + gy) * 2 * reps
            first_pass[at : at + reps, :] = re
            first_pass[at + reps : at + 2 * reps, :] = im
    for kz in range(nz):
        values = []
        for gy in range(ny):
            at = (kz * ny + gy) * 2 * reps
            values.append((first_pass[at : at + reps, :], first_pass[at + reps : at + 2 * reps, :]))
        for ky, (re, im) in enumerate(transform(values, -1)):
            t = kz * ny + ky
            put(t * reps, reps, *twisted(re, im, t, 1.0))
            mirror = (-kz % nz) * ny + (-ky % ny)
            put((parts + mirror) * reps, reps, *twisted(re, -im, mirror, 1.0))
    spectra[...] = apply(there, 2 * parts * reps)

    for t in range(parts):
        u_re, u_im = gains[t : t + 1, :], gains[parts + t : parts + t + 1, :]
        v_re = gains[2 * parts + t : 2 * parts + t + 1, :]
        v_im = gains[3 * parts + t : 3 * parts + t + 1, :]
        at, other = t * reps, (parts + t) * reps
        s_re, s_im = spectra[at : at + reps, :LANES], spectra[at : at + reps, LANES:]
        m_re, m_im = spectra[other : other + reps, :LANES], spectra[other : other + reps, LANES:]
        re = (u_re * s_re - u_im * s_im) + (v_re * m_re - v_im * m_im)
        im = (u_re * s_im + u_im * s_re) + (v_re * m_im + v_im * m_re)
        put(at, reps, re, im)
    spectra[: parts * reps, :] = apply(again, parts * reps)

    for kz in range(nz):
        values = []
        for ky in range(ny):
            t = kz * ny + ky
            at = t * reps
            re, im = spectra[at : at + reps, :LANES], spectra[at : at + reps, LANES:]
            values.append(twisted(re, im, t, -1.0))
        for gy, (re, im) in enumerate(transform(values, 1)):
            at = (kz * ny + gy) * 2 * reps
            first_pass[at : at + reps, :] = re
            first_pass[at + reps : at + 2 * reps, :] = im
    for gy in range(ny):
        values = []
        for kz in range(nz):
            at = (kz * ny + gy) * 2 * reps
            values.append((first_pass[at : at + reps, :], first_pass[at + reps : at + 2 * reps, :]))
        for gz, (re, im) in enumerate(transform(values, 1)):
            at = (gz * ny + gy) * plan.back
            out[at : at + reps, :] = re
            out[at + reps : at + 2 * reps, :] = im

    moves, _ = halo_moves(plan)
    rows, planes = plan.rows, plan.planes
    lane = lax.broadcasted_iota(jnp.int32, (SUBLANES, LANES), 1)
    comb = lane % rows

    def among(lanes):
        mask = lane < 0
        start = None
        for l in list(lanes) + [None]:
            if start is None:
                start, last = l, l
            elif l == last + 1 if l is not None else False:
                last = l
            else:
                mask = mask | ((lane >= start) & (lane <= last))
                start, last = l, l
        return mask

    masks = [among(lanes) for _, _, lanes in moves]
    before_mask = comb == 2
    last_plane = lane >= (planes - 1) * rows
    first_planes = lane < 2 * rows
    quarter = LANES // 4
    spare = (lane >= 2 * quarter) & (lane < 3 * quarter)
    pieces = plan.block // SUBLANES

    def main(gz, gy, piece):
        at = ((gz % nz) * ny + gy % ny) * plan.back + piece * SUBLANES
        return out[at : at + SUBLANES, :]

    def roll(values, shift):
        shift %= LANES
        return values if shift == 0 else pltpu.roll(values, shift, 1)

    for gy in range(ny):
        for piece in range(pieces):
            combs = [
                jnp.where(
                    before_mask,
                    roll(main(gz, gy - 1, piece), 3 - rows),
                    main(gz, gy + 1, piece),
                )
                for gz in range(nz)
            ]
            for gz in range(nz):
                corner = jnp.where(last_plane, combs[gz - 1], combs[(gz + 1) % nz])
                made = None
                for (source, shift, _), mask in zip(moves, masks):
                    moved = roll(combs[gz] if source == "own" else corner, shift)
                    made = moved if made is None else jnp.where(mask, moved, made)
                made = jnp.where(first_planes, main(gz + 1, gy, piece), made)
                made = jnp.where(last_plane, main(gz - 1, gy, piece), made)
                at = ((gz * ny + gy) * pieces + piece) * SUBLANES
                first_pass[at : at + SUBLANES, :] = made
    for s in range(parts):
        extra = first_pass[(s * pieces + pieces - 1) * SUBLANES : (s + 1) * pieces * SUBLANES, :]
        for piece, start in enumerate((0, quarter, 3 * quarter)):
            at = (s * pieces + piece) * SUBLANES
            value = first_pass[at : at + SUBLANES, :]
            to = s * plan.back + plan.block + piece * SUBLANES
            out[to : to + SUBLANES, :] = jnp.where(spare, roll(extra, 2 * quarter - start), value)


def unpack_kernel(
    plan, steps, arrived, real_table, full_table, stencil, out, inside, parts_of, coarse
):
    reps, block = plan.replicas, plan.block
    wide = 2 * LANES
    step = pl.program_id(0)

    @pl.when(step == 0)
    def _():
        lane = lax.broadcasted_iota(jnp.int32, (SUBLANES, LANES), 1)
        quarter = LANES // 4
        slot, real_at, full_at, part_at = 0, 0, 0, 0
        found = {}
        for first, modes in plan.groups:
            for m in range(len(modes)):
                at = (slot + m) * plan.back
                inside[m * block : (m + 1) * block, :LANES] = arrived[at : at + block, :]
                packed = [
                    arrived[at + block + k * SUBLANES : at + block + (k + 1) * SUBLANES, :]
                    for k in range(3)
                ]
                last = jnp.where(
                    lane < quarter,
                    pltpu.roll(packed[0], 2 * quarter, 1),
                    jnp.where(
                        lane < 2 * quarter,
                        pltpu.roll(packed[1], 3 * quarter, 1),
                        pltpu.roll(packed[2], quarter, 1),
                    ),
                )
                for k, value in enumerate(packed + [last]):
                    to = m * block + k * SUBLANES
                    inside[to : to + SUBLANES, LANES:] = value
            depth = len(modes) * block
            high, low = split(inside[:depth, :])
            both = jnp.concatenate([high, low, high], axis=0)
            if first in (0, plan.radix // 2):
                size, table, at = LANES, real_table, real_at
                real_at += size
            else:
                size, table, at = 2 * LANES, full_table, full_at
                full_at += size
            w_high = table[at : at + size, :depth]
            w_low = table[at : at + size, depth:]
            made = dot(jnp.concatenate([w_high, w_high, w_low], axis=1), both, NN)
            parts_of[part_at : part_at + size, :] = made
            found[first] = (part_at, size > LANES)
            part_at += size
            slot += len(modes)
        for x_l in range(plan.fine_x):
            for piece in range(reps // SUBLANES):
                row = x_l * reps + piece * SUBLANES
                values = []
                for first in range(plan.radix // 2 + 1):
                    at, is_full = found[first]
                    re = parts_of[at + row : at + row + SUBLANES, :]
                    im = None
                    if is_full:
                        im = parts_of[at + LANES + row : at + LANES + row + SUBLANES, :]
                    values.append((re, im))
                for xh, value in enumerate(to_real(values)):
                    x = xh * plan.fine_x + x_l
                    places = [x + 1]
                    if x == plan.count - 1:
                        places.append(0)
                    if x < 2:
                        places.append(x + 1 + plan.count)
                    for place in places:
                        to = place * reps + piece * SUBLANES
                        coarse[to : to + SUBLANES, :] = value

    here = plan.count // steps
    made = []
    for i in range(here):
        taps = []
        for move in range(4):
            at = pl.multiple_of((step * here + i + move) * reps, reps)
            taps.append(coarse[pl.ds(at, reps), :])
        made.append(taps[1])
        made.append((taps[1] + taps[2]) * (9.0 / 16.0) - (taps[0] + taps[3]) * (1.0 / 16.0))
    high, low = split(jnp.concatenate(made, axis=0))
    table = stencil[...]
    fine = dot(
        jnp.concatenate([table, table], axis=1), jnp.concatenate([high, low], axis=1), NT
    )
    out[...] = fine.reshape(out.shape)


def exchanged(values, parts):
    rows = values.shape[0]
    values = values.reshape(parts, 1, rows // parts * LANES)
    values = lax.all_to_all(values, ("gz", "gy"), split_axis=0, concat_axis=0, tiled=True)
    return values.reshape(rows, LANES)


def fast_form(plan, charges, kernel):
    f32, bf16 = jnp.float32, jnp.bfloat16
    parts, reps, block = plan.parts, plan.replicas, plan.block
    limit = pltpu.CompilerParams(vmem_limit_bytes=40 * 1024 * 1024)
    tables = [jnp.asarray(t) for t in pack_tables(plan)]
    packed = pl.pallas_call(
        functools.partial(pack_kernel, plan),
        out_shape=jax.ShapeDtypeStruct((parts * plan.sent, LANES), f32),
        in_specs=[VMEM] * 5,
        out_specs=VMEM,
        compiler_params=limit,
        name="pack",
    )(charges, kernel, *tables)
    packed = exchanged(packed, parts)

    me = lax.axis_index("gz") * plan.ny + lax.axis_index("gy")
    tables = [jnp.asarray(t) for t in plane_tables(plan)]
    planes = pl.pallas_call(
        functools.partial(plane_kernel, plan),
        out_shape=jax.ShapeDtypeStruct((parts * plan.back, LANES), f32),
        in_specs=[pl.BlockSpec(memory_space=pltpu.SMEM)] + [VMEM] * 5,
        out_specs=VMEM,
        scratch_shapes=[
            pltpu.VMEM((parts * block, LANES), f32),
            pltpu.VMEM((2 * parts * reps, 2 * LANES), f32),
            pltpu.VMEM((4 * parts, LANES), f32),
            pltpu.VMEM((2 * parts * reps, 2 * LANES), bf16),
            pltpu.VMEM((2 * parts * reps, 2 * LANES), bf16),
        ],
        compiler_params=limit,
        name="plane",
    )(me.reshape(1), packed, *tables)
    planes = exchanged(planes, parts)

    steps = 4
    fine_shape = (2 * plan.planes, 2 * plan.rows, 2 * plan.count * reps)
    tables = [jnp.asarray(t) for t in unpack_tables(plan)]
    fixed = lambda shape: pl.BlockSpec(shape, lambda j: (0,) * len(shape))
    operands = (planes, *tables, jnp.asarray(stencil_table(plan)))
    return pl.pallas_call(
        functools.partial(unpack_kernel, plan, steps),
        out_shape=jax.ShapeDtypeStruct(fine_shape, f32),
        grid=(steps,),
        in_specs=[fixed(o.shape) for o in operands],
        out_specs=pl.BlockSpec(fine_shape[:2] + (fine_shape[2] // steps,), lambda j: (0, 0, j)),
        scratch_shapes=[
            pltpu.VMEM((2 * LANES, 2 * LANES), f32),
            pltpu.VMEM((plan.radix * LANES, 2 * LANES), f32),
            pltpu.VMEM(((plan.count + 3) * reps, 2 * LANES), f32),
        ],
        compiler_params=limit,
        name="unpack",
    )(*operands)


def extended(block, sides, width):
    for axis, dim in sides:
        count = lax.axis_size(axis)
        forward_pairs = [(i, (i + 1) % count) for i in range(count)]
        backward_pairs = [(target, source) for source, target in forward_pairs]
        low = lax.ppermute(
            lax.slice_in_dim(block, block.shape[dim] - width, None, axis=dim), axis, forward_pairs
        )
        high = lax.ppermute(lax.slice_in_dim(block, 0, width, axis=dim), axis, backward_pairs)
        block = jnp.concatenate([low, block, high], axis=dim)
    return block


def tables_of(count):
    index = jnp.arange(count, dtype=jnp.int32)
    product = index[:, None] * index[None, :] % count
    angle = product.astype(jnp.float32) * (2.0 * math.pi / count)
    return (jnp.cos(angle), jnp.sin(angle))


def along(values, table, axis):
    moved = jnp.tensordot(values, table, axes=((axis,), (0,)), precision=lax.Precision.HIGHEST)
    return jnp.moveaxis(moved, -1, axis)


def forward(spectrum, axis, cosines, sines):
    real_part, imag_part = (spectrum[0], spectrum[1])
    inner = axis - 1
    new_real = along(real_part, cosines, inner) + along(imag_part, sines, inner)
    new_imag = along(imag_part, cosines, inner) - along(real_part, sines, inner)
    return jnp.stack([new_real, new_imag])


def backward(spectrum, axis, cosines, sines):
    real_part, imag_part = (spectrum[0], spectrum[1])
    inner = axis - 1
    count = cosines.shape[0]
    new_real = (along(real_part, cosines, inner) - along(imag_part, sines, inner)) / count
    new_imag = (along(imag_part, cosines, inner) + along(real_part, sines, inner)) / count
    return jnp.stack([new_real, new_imag])


def refine_rim(haloed, axis, count):
    centre = lax.slice_in_dim(haloed, 2, 2 + count, axis=axis)
    before = lax.slice_in_dim(haloed, 1, 1 + count, axis=axis)
    after = lax.slice_in_dim(haloed, 3, 3 + count, axis=axis)
    after_two = lax.slice_in_dim(haloed, 4, 4 + count, axis=axis)
    middle = (9.0 * (centre + after) - (before + after_two)) / 16.0
    stacked = jnp.stack([centre, middle], axis=axis + 1)
    shape = list(centre.shape)
    shape[axis] = 2 * count
    return stacked.reshape(shape)


def refine_loop(coarse, axis):
    before = jnp.roll(coarse, 1, axis)
    after = jnp.roll(coarse, -1, axis)
    after_two = jnp.roll(coarse, -2, axis)
    middle = (9.0 * (coarse + after) - (before + after_two)) / 16.0
    stacked = jnp.stack([coarse, middle], axis=axis + 1)
    shape = list(coarse.shape)
    shape[axis] = 2 * shape[axis]
    return stacked.reshape(shape)


def general_form(charges, kernel):
    planes, rows, count = (kernel.shape[0], kernel.shape[1], kernel.shape[2])
    replicas = charges.shape[2] // count
    grids = charges.reshape(planes, rows, count, replicas)
    cosines, sines = tables_of(count)
    spectrum = jnp.stack([along(grids, cosines, 2), -along(grids, sines, 2)])
    kernel_spec = jnp.stack([along(kernel, cosines, 2), -along(kernel, sines, 2)])
    spectrum, kernel_spec = (
        lax.all_to_all(spectrum, "gy", split_axis=3, concat_axis=2, tiled=True),
        lax.all_to_all(kernel_spec, "gy", split_axis=3, concat_axis=2, tiled=True),
    )
    spectrum = forward(spectrum, 2, cosines, sines)
    kernel_spec = forward(kernel_spec, 2, cosines, sines)
    spectrum, kernel_spec = (
        lax.all_to_all(spectrum, "gz", split_axis=2, concat_axis=1, tiled=True),
        lax.all_to_all(kernel_spec, "gz", split_axis=2, concat_axis=1, tiled=True),
    )
    spectrum = forward(spectrum, 1, cosines, sines)
    kernel_spec = forward(kernel_spec, 1, cosines, sines)
    kernel_real = kernel_spec[0][..., None]
    kernel_imag = kernel_spec[1][..., None]
    product_real = spectrum[0] * kernel_real - spectrum[1] * kernel_imag
    product_imag = spectrum[1] * kernel_real + spectrum[0] * kernel_imag
    spectrum = backward(jnp.stack([product_real, product_imag]), 1, cosines, sines)
    spectrum = lax.all_to_all(spectrum, "gz", split_axis=1, concat_axis=2, tiled=True)
    spectrum = backward(spectrum, 2, cosines, sines)
    spectrum = lax.all_to_all(spectrum, "gy", split_axis=2, concat_axis=3, tiled=True)
    potential = (along(spectrum[0], cosines, 2) - along(spectrum[1], sines, 2)) / count
    haloed = extended(potential, (("gz", 0), ("gy", 1)), 2)
    result = refine_rim(haloed, 0, planes)
    result = refine_rim(result, 1, rows)
    result = refine_loop(result, 2)
    return result.reshape(2 * planes, 2 * rows, 2 * count * replicas)


def per_device(nz, ny, charges, kernel):
    planes, rows, count = kernel.shape
    replicas = charges.shape[2] // count
    sizes = (planes, rows, count, replicas, nz, ny)
    if Plan.fits(*sizes):
        return fast_form(Plan(*sizes), charges, kernel)
    return general_form(charges, kernel)


def solution(mesh):
    placed = (P("gz", "gy", None), P("gz", "gy", None))
    sizes = (mesh.shape["gz"], mesh.shape["gy"])
    return jax.shard_map(
        functools.partial(per_device, *sizes),
        mesh=mesh,
        in_specs=placed,
        out_specs=P("gz", "gy", None),
        check_vma=False,
    )
```

profile of v0, /device:TPU:0, one launch (start us, length us, event | category | flops | bytes accessed | tf_op | source)
XLA Modules:
  0.0 66.4 jit_solution(14221039610289934988)
XLA Ops:
  0.0 0.0 copy-start
  0.0 0.0 copy-start.1
  0.0 1.2 %copy-done.1 = bf16[768,512]{1,0:T(8,128)(2,1)S(1)} copy-done((bf16[768,512]{1,0:T(8,128)(2,1)S(1)}, bf16[768,512]{1,0:T(8,128)(2,1)}, u32[]{:S(2)}) %copy-start.1) | copy-done | bytes 786456
  1.2 0.0 copy-start.2
  1.2 1.0 %copy-done.2 = f32[8,16,1024]{2,1,0:T(8,128)S(1)} copy-done((f32[8,16,1024]{2,1,0:T(8,128)S(1)}, f32[8,16,1024]{2,1,0:T(8,128)}, u32[]{:S(2)}) %copy-start.2) | copy-done | bytes 524312
  2.3 0.0 copy-start.7
  2.3 0.9 %copy-done.7 = bf16[256,256]{1,0:T(8,128)(2,1)S(1)} copy-done((bf16[256,256]{1,0:T(8,128)(2,1)S(1)}, bf16[256,256]{1,0:T(8,128)(2,1)}, u32[]{:S(2)}) %copy-start.7) | copy-done | bytes 131096
  3.2 0.0 copy-start.8
  3.2 0.8 %copy-done.8 = f32[8,16,64]{2,1,0:T(8,128)S(1)} copy-done((f32[8,16,64]{2,1,0:T(8,128)S(1)}, f32[8,16,64]{2,1,0:T(8,128)}, u32[]{:S(2)}) %copy-start.8) | copy-done | bytes 32792
  4.0 0.0 copy-start.11
  4.0 0.8 %copy-done.11 = f32[64,64]{1,0:T(8,128)S(1)} copy-done((f32[64,64]{1,0:T(8,128)S(1)}, f32[64,64]{1,0:T(8,128)}, u32[]{:S(2)}) %copy-start.11) | copy-done | bytes 16408
  4.8 0.0 copy-start.3
  4.8 0.0 copy-start.6
  4.8 1.5 %pack.1 = f32[1088,128]{1,0:T(8,128)} custom-call(f32[8,16,1024]{2,1,0:T(8,128)S(1)} %copy-done.2, f32[8,16,64]{2,1,0:T(8,128)S(1)} %copy-done.8, bf16[256,256]{1,0:T(8,128)(2,1)S(1)} %copy-done.7, bf16[768,512]{1,0:T(8,128)(2,1)S(1)} %copy-done.1, f32[64,64]{1,0:T(8,128)S(1)} %copy-done.11), custom_call_target="tpu_custom_call" | custom-call | tf_op jit(solution)/shard_map/pack/pallas_call | solution.py:600
  6.2 7.3 %all-to-all-start = ((f32[32,1,4352]{2,1,0:T(1,128)}), f32[32,1,4352]{2,1,0:T(1,128)S(1)}, u32[]{:S(2)}, u32[]{:S(2)}) async-start(f32[32,1,4352]{2,1,0:T(1,128)} %bitcast.1), calls=%async_computation | async-start | bytes 1114112 | tf_op jit(solution)/shard_map/all_to_all | solution.py:591
  13.6 16.2 %all-to-all-done = f32[32,1,4352]{2,1,0:T(1,128)S(1)} async-done(((f32[32,1,4352]{2,1,0:T(1,128)}), f32[32,1,4352]{2,1,0:T(1,128)S(1)}, u32[]{:S(2)}, u32[]{:S(2)}) %all-to-all-start) | async-done | bytes 557088 | tf_op jit(solution)/shard_map/all_to_all | solution.py:591
  29.8 0.0 copy-start.4
  29.8 0.9 %copy-done.4 = bf16[256,512]{1,0:T(8,128)(2,1)S(1)} copy-done((bf16[256,512]{1,0:T(8,128)(2,1)S(1)}, bf16[256,512]{1,0:T(8,128)(2,1)}, u32[]{:S(2)}) %copy-start.4) | copy-done | bytes 262168
  30.7 0.0 copy-start.5
  30.7 0.9 %copy-done.5 = bf16[256,512]{1,0:T(8,128)(2,1)S(1)} copy-done((bf16[256,512]{1,0:T(8,128)(2,1)S(1)}, bf16[256,512]{1,0:T(8,128)(2,1)}, u32[]{:S(2)}) %copy-start.5) | copy-done | bytes 262168
  31.7 0.0 copy-start.9
  31.7 0.8 %copy-done.9 = f32[128,64]{1,0:T(8,128)S(1)} copy-done((f32[128,64]{1,0:T(8,128)S(1)}, f32[128,64]{1,0:T(8,128)}, u32[]{:S(2)}) %copy-start.9) | copy-done | bytes 32792
  32.5 0.0 copy-start.10
  32.5 0.8 %copy-done.10 = f32[64,128]{1,0:T(8,128)S(1)} copy-done((f32[64,128]{1,0:T(8,128)S(1)}, f32[64,128]{1,0:T(8,128)}, u32[]{:S(2)}) %copy-start.10) | copy-done | bytes 32792
  33.3 2.6 %plane.1 = f32[1792,128]{1,0:T(8,128)S(1)} custom-call(s32[1]{0:T(128)} %bitcast.shared, f32[1088,128]{1,0:T(8,128)S(1)} %bitcast.7, f32[64,128]{1,0:T(8,128)S(1)} %copy-done.10, bf16[256,512]{1,0:T(8,128)(2,1)S(1)} %copy-done.5, bf16[256,512]{1,0:T(8,128)(2,1)S(1)} %copy-done.4, f32[128,64]{1,0:T(8,128)S(1)} %copy-done.9), custom_call_target="tpu_custom_call" | custom-call | tf_op jit(solution)/shard_map/plane/pallas_call | solution.py:612
  35.9 26.3 %all_to_all.10 = f32[32,1,7168]{2,1,0:T(1,128)S(1)} all-to-all(f32[32,1,7168]{2,1,0:T(1,128)S(1)} %bitcast.6), channel_id=1, replica_groups=mesh['gz'=8,'gy'=4] {'gz','gy'}, dimensions={0} | all-to-all | bytes 1835008 | tf_op jit(solution)/shard_map/all_to_all | solution.py:591
  62.2 0.0 copy-done
  62.2 0.0 copy-done.3
  62.2 0.0 copy-done.6
  62.2 4.1 %unpack.1 = f32[16,32,2048]{2,1,0:T(8,128)} custom-call(f32[1792,128]{1,0:T(8,128)S(1)} %bitcast.5, bf16[256,256]{1,0:T(8,128)(2,1)S(1)} %copy-done.6, bf16[768,512]{1,0:T(8,128)(2,1)S(1)} %copy-done, bf16[512,256]{1,0:T(8,128)(2,1)S(1)} %copy-done.3), custom_call_target="tpu_custom_call" | custom-call | tf_op jit(solution)/shard_map/unpack/pallas_call | solution.py:634
Async XLA Ops:
  0.0 62.2 %copy-start = (bf16[768,512]{1,0:T(8,128)(2,1)S(1)}, bf16[768,512]{1,0:T(8,128)(2,1)}, u32[]{:S(2)}) copy-start(bf16[768,512]{1,0:T(8,128)(2,1)} %constant.39.clone.full_table) | copy-start | bytes 2359300
  0.0 1.2 %copy-start.1 = (bf16[768,512]{1,0:T(8,128)(2,1)S(1)}, bf16[768,512]{1,0:T(8,128)(2,1)}, u32[]{:S(2)}) copy-start(bf16[768,512]{1,0:T(8,128)(2,1)} %constant.32.clone.full_table) | copy-start | bytes 2359300
  1.2 1.0 %copy-start.2 = (f32[8,16,1024]{2,1,0:T(8,128)S(1)}, f32[8,16,1024]{2,1,0:T(8,128)}, u32[]{:S(2)}) copy-start(f32[8,16,1024]{2,1,0:T(8,128)} %charges.1) | copy-start | bytes 1572868
  2.3 0.9 %copy-start.7 = (bf16[256,256]{1,0:T(8,128)(2,1)S(1)}, bf16[256,256]{1,0:T(8,128)(2,1)}, u32[]{:S(2)}) copy-start(bf16[256,256]{1,0:T(8,128)(2,1)} %constant.31.clone.real_table) | copy-start | bytes 393220
  3.2 0.8 %copy-start.8 = (f32[8,16,64]{2,1,0:T(8,128)S(1)}, f32[8,16,64]{2,1,0:T(8,128)}, u32[]{:S(2)}) copy-start(f32[8,16,64]{2,1,0:T(8,128)} %kernel.1) | copy-start | bytes 98308
  4.0 0.8 %copy-start.11 = (f32[64,64]{1,0:T(8,128)S(1)}, f32[64,64]{1,0:T(8,128)}, u32[]{:S(2)}) copy-start(f32[64,64]{1,0:T(8,128)} %constant.33.clone.kernel_table) | copy-start | bytes 49156
  4.8 57.5 %copy-start.3 = (bf16[512,256]{1,0:T(8,128)(2,1)S(1)}, bf16[512,256]{1,0:T(8,128)(2,1)}, u32[]{:S(2)}) copy-start(bf16[512,256]{1,0:T(8,128)(2,1)} %constant.40.clone.stencil) | copy-start | bytes 786436
  4.8 57.5 %copy-start.6 = (bf16[256,256]{1,0:T(8,128)(2,1)S(1)}, bf16[256,256]{1,0:T(8,128)(2,1)}, u32[]{:S(2)}) copy-start(bf16[256,256]{1,0:T(8,128)(2,1)} %constant.38.clone.real_table) | copy-start | bytes 393220
  6.2 23.5 %all-to-all-start = ((f32[32,1,4352]{2,1,0:T(1,128)}), f32[32,1,4352]{2,1,0:T(1,128)S(1)}, u32[]{:S(2)}, u32[]{:S(2)}) async-start(f32[32,1,4352]{2,1,0:T(1,128)} %bitcast.1), calls=%async_computation | async-start | bytes 1114112 | tf_op jit(solution)/shard_map/all_to_all | solution.py:591
  29.8 1.0 %copy-start.4 = (bf16[256,512]{1,0:T(8,128)(2,1)S(1)}, bf16[256,512]{1,0:T(8,128)(2,1)}, u32[]{:S(2)}) copy-start(bf16[256,512]{1,0:T(8,128)(2,1)} %constant.36.clone.again) | copy-start | bytes 786436
  30.7 0.9 %copy-start.5 = (bf16[256,512]{1,0:T(8,128)(2,1)S(1)}, bf16[256,512]{1,0:T(8,128)(2,1)}, u32[]{:S(2)}) copy-start(bf16[256,512]{1,0:T(8,128)(2,1)} %constant.35.clone.there) | copy-start | bytes 786436
  31.7 0.8 %copy-start.9 = (f32[128,64]{1,0:T(8,128)S(1)}, f32[128,64]{1,0:T(8,128)}, u32[]{:S(2)}) copy-start(f32[128,64]{1,0:T(8,128)} %constant.37.clone.blocks) | copy-start | bytes 98308
  32.5 0.8 %copy-start.10 = (f32[64,128]{1,0:T(8,128)S(1)}, f32[64,128]{1,0:T(8,128)}, u32[]{:S(2)}) copy-start(f32[64,128]{1,0:T(8,128)} %constant.34.clone.twist) | copy-start | bytes 98308
where the time goes:
time: 66.9 us; the launch traced here: 66.4 us
  blocking collectives  26.3 us (39%)
  waiting for transfers between devices  16.2 us (24%)
  local copies, waits for them, and re-layouts  8.25 us (12%)
  Pallas kernels  8.24 us (12%)
  starting transfers between devices  7.33 us (11%)
    all_to_all x1, blocking collectives, exchanged(): lax.all_to_all(values, ('gz', 'gy'), split_axis=0, concat_axis=0, tiled=T...  26.3 us
    all_to_all x1, waiting for transfers between devices, exchanged(): lax.all_to_all(values, ('gz', 'gy'), split_axis=0, concat_axis=0, tiled=T...  16.2 us
    unnamed x24, local copies, waits for them, and re-layouts  8.25 us
    all_to_all x1, starting transfers between devices, exchanged(): lax.all_to_all(values, ('gz', 'gy'), split_axis=0, concat_axis=0, tiled=T...  7.33 us
    pallas_call x1, Pallas kernels, fast_form(): pl.pallas_call(functools.partial(unpack_kernel, plan, steps), out_shape=j...  4.13 us
    pallas_call x1, Pallas kernels, fast_form(): pl.pallas_call(functools.partial(plane_kernel, plan), out_shape=jax.Shape...  2.65 us
    pallas_call x1, Pallas kernels, fast_form(): pl.pallas_call(functools.partial(pack_kernel, plan), out_shape=jax.ShapeD...  1.46 us
  transfers between devices with their start and end apart: 1, of which 1 were waited for; matrix products, arithmetic and copies ran while one was open for 0% of the time, Pallas kernels for 0%

commit v1 on v0

--- a/solution.py
+++ b/solution.py
@@ -13,6 +13,8 @@
 SUBLANES = 8
 TAPS = ((-1, -1.0 / 16.0), (0, 9.0 / 16.0), (1, 9.0 / 16.0), (2, -1.0 / 16.0))
 VMEM = pl.BlockSpec(memory_space=pltpu.VMEM)
+SMEM = pl.BlockSpec(memory_space=pltpu.SMEM)
+HBM = pl.BlockSpec(memory_space=pltpu.HBM)
 NT = (((1,), (1,)), ((), ()))
 NN = (((1,), (0,)), ((), ()))
 
@@ -125,7 +127,7 @@
     angle = 2 * np.pi * (np.outer(z_of, z_of) / plan.nz + np.outer(y_of, y_of) / plan.ny)
     cosine, sine = np.cos(angle), np.sin(angle)
     blocks = np.block([[cosine, sine], [-sine, cosine], [cosine, -sine], [-sine, -cosine]])
-    return twist, side_by_side(there), side_by_side(again), blocks.astype(np.float32)
+    return twist, blocks.astype(np.float32), side_by_side(there), side_by_side(again)
 
 
 def halo_moves(plan):
@@ -297,13 +299,37 @@
     return made
 
 
-def pack_kernel(plan, charges, kernel, real_table, full_table, kernel_table, out):
+def fetches(sources, targets, arrivals):
+    copies = [
+        pltpu.make_async_copy(source, target, arrivals.at[i])
+        for i, (source, target) in enumerate(zip(sources, targets))
+    ]
+    for copy in copies:
+        copy.start()
+    return copies
+
+
+def room_for(operands):
+    return [pltpu.VMEM(o.shape, o.dtype) for o in operands] + [
+        pltpu.SemaphoreType.DMA((len(operands),))
+    ]
+
+
+def pack_kernel(plan, ahead, _, *refs):
+    sources, later = refs[:5], refs[5 : 5 + ahead]
+    out, carried = refs[5 + ahead], refs[6 + ahead : 6 + 2 * ahead]
+    targets, arrivals, others = refs[-7:-2], refs[-2], refs[-1]
+    copies = fetches(sources, targets, arrivals)
+    later_copies = fetches(later, carried, others)
+    charges, kernel, real_table, full_table, kernel_table = targets
     width, block = LANES, plan.block
+    copies[0].wait()
     tiles = [
         charges[:, :, a * width : (a + 1) * width].reshape(LANES, width)
         for a in range(plan.radix)
     ]
     spectrum = from_real(tiles)
+    copies[2].wait()
     slot, real_at, full_at = 0, 0, 0
     for first, modes in plan.groups:
         re, im = spectrum[first]
@@ -313,6 +339,8 @@
             real_at += size
             values = re
         else:
+            if full_at == 0:
+                copies[3].wait()
             columns, table, at = 2 * width, full_table, full_at
             full_at += size
             values = jnp.concatenate([re, im], axis=1)
@@ -328,16 +356,21 @@
             start = (slot + m) * plan.sent
             out[start : start + block, :] = made[m * block : (m + 1) * block]
         slot += len(modes)
+    copies[1].wait()
+    copies[4].wait()
     made = dot_exact(kernel_table[...], kernel[...].reshape(LANES, plan.count), NT)
     for c in range(2):
         rows = pl.ds(block + c, plan.parts, stride=plan.sent)
         out[rows, :] = made[c * plan.parts : (c + 1) * plan.parts]
-
-
-def plane_kernel(
-    plan, shared, arrived, twist, there, again, blocks, out,
-    first_pass, spectra, gains, high_part, low_part,
-):
+    for copy in later_copies:
+        copy.wait()
+
+
+def plane_kernel(plan, ahead, shared, arrived, *refs):
+    twist, blocks, there, again = refs[:4]
+    later, out, carried = refs[4 : 4 + ahead], refs[4 + ahead], refs[5 + ahead : 5 + 2 * ahead]
+    first_pass, spectra, gains, high_part, low_part, others = refs[-6:]
+    later_copies = fetches(later, carried, others)
     nz, ny, parts, reps = plan.nz, plan.ny, plan.parts, plan.replicas
     whole = 2 * LANES
 
@@ -359,6 +392,15 @@
         high_part[at : at + size, :] = high
         low_part[at : at + size, :] = low
 
+    for gy in range(ny):
+        values = []
+        for gz in range(nz):
+            at = (gz * ny + gy) * plan.sent
+            values.append((arrived[at : at + reps, :], arrived[at + reps : at + 2 * reps, :]))
+        for kz, (re, im) in enumerate(transform(values, -1)):
+            at = (kz * ny + gy) * 2 * reps
+            first_pass[at : at + reps, :] = re
+            first_pass[at + reps : at + 2 * reps, :] = im
     lines = jnp.concatenate(
         [arrived[pl.ds(plan.block + c, parts, stride=plan.sent), :] for c in range(2)]
     )
@@ -380,15 +422,6 @@
     gains[2 * parts : 3 * parts, :] = jnp.where(is_shared, 0.5 * (a_re - b_re), zero)
     gains[3 * parts : 4 * parts, :] = jnp.where(is_shared, 0.5 * (a_im - b_im), zero)
 
-    for gy in range(ny):
-        values = []
-        for gz in range(nz):
-            at = (gz * ny + gy) * plan.sent
-            values.append((arrived[at : at + reps, :], arrived[at + reps : at + 2 * reps, :]))
-        for kz, (re, im) in enumerate(transform(values, -1)):
-            at = (kz * ny + gy) * 2 * reps
-            first_pass[at : at + reps, :] = re
-            first_pass[at + reps : at + 2 * reps, :] = im
     for kz in range(nz):
         values = []
         for gy in range(ny):
@@ -495,6 +528,8 @@
             value = first_pass[at : at + SUBLANES, :]
             to = s * plan.back + plan.block + piece * SUBLANES
             out[to : to + SUBLANES, :] = jnp.where(spare, roll(extra, 2 * quarter - start), value)
+    for copy in later_copies:
+        copy.wait()
 
 
 def unpack_kernel(
@@ -592,45 +627,56 @@
     return values.reshape(rows, LANES)
 
 
+def in_hbm(arrays):
+    return [pltpu.with_memory_space_constraint(array, pltpu.HBM) for array in arrays]
+
+
+def like(arrays):
+    return [jax.ShapeDtypeStruct(array.shape, array.dtype) for array in arrays]
+
+
 def fast_form(plan, charges, kernel):
     f32, bf16 = jnp.float32, jnp.bfloat16
     parts, reps, block = plan.parts, plan.replicas, plan.block
     limit = pltpu.CompilerParams(vmem_limit_bytes=40 * 1024 * 1024)
-    tables = [jnp.asarray(t) for t in pack_tables(plan)]
-    packed = pl.pallas_call(
-        functools.partial(pack_kernel, plan),
-        out_shape=jax.ShapeDtypeStruct((parts * plan.sent, LANES), f32),
-        in_specs=[VMEM] * 5,
-        out_specs=VMEM,
+    me = (lax.axis_index("gz") * plan.ny + lax.axis_index("gy")).reshape(1)
+
+    operands = [charges, kernel] + [jnp.asarray(t) for t in pack_tables(plan)]
+    tables = [jnp.asarray(t) for t in plane_tables(plan)]
+    packed, *tables = pl.pallas_call(
+        functools.partial(pack_kernel, plan, len(tables)),
+        out_shape=[jax.ShapeDtypeStruct((parts * plan.sent, LANES), f32)] + like(tables),
+        in_specs=[SMEM] + [HBM] * (len(operands) + len(tables)),
+        out_specs=[VMEM] * (1 + len(tables)),
+        scratch_shapes=room_for(operands) + [pltpu.SemaphoreType.DMA((len(tables),))],
         compiler_params=limit,
         name="pack",
-    )(charges, kernel, *tables)
+    )(me, *in_hbm(operands), *in_hbm(tables))
     packed = exchanged(packed, parts)
 
-    me = lax.axis_index("gz") * plan.ny + lax.axis_index("gy")
-    tables = [jnp.asarray(t) for t in plane_tables(plan)]
-    planes = pl.pallas_call(
-        functools.partial(plane_kernel, plan),
-        out_shape=jax.ShapeDtypeStruct((parts * plan.back, LANES), f32),
-        in_specs=[pl.BlockSpec(memory_space=pltpu.SMEM)] + [VMEM] * 5,
-        out_specs=VMEM,
+    later = [jnp.asarray(t) for t in unpack_tables(plan) + (stencil_table(plan),)]
+    planes, *later = pl.pallas_call(
+        functools.partial(plane_kernel, plan, len(later)),
+        out_shape=[jax.ShapeDtypeStruct((parts * plan.back, LANES), f32)] + like(later),
+        in_specs=[SMEM] + [VMEM] * (1 + len(tables)) + [HBM] * len(later),
+        out_specs=[VMEM] * (1 + len(later)),
         scratch_shapes=[
             pltpu.VMEM((parts * block, LANES), f32),
             pltpu.VMEM((2 * parts * reps, 2 * LANES), f32),
             pltpu.VMEM((4 * parts, LANES), f32),
             pltpu.VMEM((2 * parts * reps, 2 * LANES), bf16),
             pltpu.VMEM((2 * parts * reps, 2 * LANES), bf16),
+            pltpu.SemaphoreType.DMA((len(later),)),
         ],
         compiler_params=limit,
         name="plane",
-    )(me.reshape(1), packed, *tables)
+    )(me, packed, *tables, *in_hbm(later))
     planes = exchanged(planes, parts)
 
     steps = 4
     fine_shape = (2 * plan.planes, 2 * plan.rows, 2 * plan.count * reps)
-    tables = [jnp.asarray(t) for t in unpack_tables(plan)]
     fixed = lambda shape: pl.BlockSpec(shape, lambda j: (0,) * len(shape))
-    operands = (planes, *tables, jnp.asarray(stencil_table(plan)))
+    operands = (planes, *later)
     return pl.pallas_call(
         functools.partial(unpack_kernel, plan, steps),
         out_shape=jax.ShapeDtypeStruct(fine_shape, f32),

time: 66.9 us -> 59 us (0.88)
  blocking collectives: 26.3 us -> 49.6 us
  waiting for transfers between devices: 16.2 us -> 0 us
  local copies, waits for them, and re-layouts: 8.25 us -> 0 us
  starting transfers between devices: 7.33 us -> 0 us
  Pallas kernels: 8.24 us -> 9.2 us
    all_to_all x1 -> x2, blocking collectives: 26.3 us -> 49.6 us  [exchanged(): lax.all_to_all(values, ('gz', 'gy'), split_axis=0, concat_axis=0, tiled=T...]
    all_to_all x1 -> x0, waiting for transfers between devices: 16.2 us -> none  [exchanged(): lax.all_to_all(values, ('gz', 'gy'), split_axis=0, concat_axis=0, tiled=T...]
    unnamed x24 -> x0, local copies, waits for them, and re-layouts: 8.25 us -> none
    all_to_all x1 -> x0, starting transfers between devices: 7.33 us -> none  [exchanged(): lax.all_to_all(values, ('gz', 'gy'), split_axis=0, concat_axis=0, tiled=T...]
    pallas_call x2, Pallas kernels: 4.11 us -> 5.07 us  [the longest x1 2.68 us: fast_form(): pl.pallas_call(functools.partial(plane_kernel, plan, len(later)), out_sha...]
  transfers between devices with their start and end apart: 1 -> 0, of which waited for: 1 -> 0; matrix products, arithmetic and copies ran while one was open for 0% -> 0% of each run, Pallas kernels for 0% -> 0%
where the time goes in v1:
time: 59 us; the launch traced here: 58.8 us
  blocking collectives  49.6 us (84%)
  Pallas kernels  9.2 us (16%)
    all_to_all x2, blocking collectives, exchanged(): lax.all_to_all(values, ('gz', 'gy'), split_axis=0, concat_axis=0, tiled=T...  49.6 us
    pallas_call x1, Pallas kernels, fast_form(): pl.pallas_call(functools.partial(unpack_kernel, plan, steps), out_shape=j...  4.13 us
    pallas_call x1, Pallas kernels, fast_form(): pl.pallas_call(functools.partial(plane_kernel, plan, len(later)), out_sha...  2.68 us
    pallas_call x1, Pallas kernels, fast_form(): pl.pallas_call(functools.partial(pack_kernel, plan, len(tables)), out_sha...  2.38 us

profile of v1, /device:TPU:0, one launch (start us, length us, event | category | flops | bytes accessed | tf_op | source)
XLA Modules:
  0.0 58.8 jit_solution(16650972808769898040)
XLA Ops:
  0.0 2.4 %pack.1 = (f32[1088,128]{1,0:T(8,128)S(1)}, f32[64,128]{1,0:T(8,128)S(1)}, f32[128,64]{1,0:T(8,128)S(1)}, bf16[256,512]{1,0:T(8,128)(2,1)S(1)}, bf16[256,512]{1,0:T(8,128)(2,1)S(1)}) custom-call(s32[1]{0:T(128)} %bitcast._.shared, f32[8,16,1024]{2,1,0:T(8,128)} %refs_0_.1, f32[8,16,64]{2,1,0:T(8,128)} %refs_1_.1, bf16[256,256]{1,0:T(8,128)(2,1)} %constant.31.clone.refs_2_, ...), custom_call_target="tpu_custom_call" | custom-call | tf_op jit(solution)/shard_map/pack/pallas_call | solution.py:646
  2.4 23.3 %all_to_all.10 = f32[32,1,4352]{2,1,0:T(1,128)S(1)} all-to-all(f32[32,1,4352]{2,1,0:T(1,128)S(1)} %bitcast.8), channel_id=1, replica_groups=mesh['gz'=8,'gy'=4] {'gz','gy'}, dimensions={0} | all-to-all | bytes 1114112 | tf_op jit(solution)/shard_map/all_to_all | solution.py:626
  25.7 2.7 %plane.1 = (f32[1792,128]{1,0:T(8,128)S(1)}, bf16[256,256]{1,0:T(8,128)(2,1)S(1)}, bf16[768,512]{1,0:T(8,128)(2,1)S(1)}, bf16[512,256]{1,0:T(8,128)(2,1)S(1)}) custom-call(s32[1]{0:T(128)} %bitcast._.shared, f32[1088,128]{1,0:T(8,128)S(1)} %bitcast.6, f32[64,128]{1,0:T(8,128)S(1)} %get-tuple-element.15.refs_0_, f32[128,64]{1,0:T(8,128)S(1)} %get-tuple-element.16.refs_1_, ...), custom_call_target="tpu_custom_call" | custom-call | tf_op jit(solution)/shard_map/plane/pallas_call | solution.py:658
  28.4 26.3 %all_to_all.11 = f32[32,1,7168]{2,1,0:T(1,128)S(1)} all-to-all(f32[32,1,7168]{2,1,0:T(1,128)S(1)} %bitcast.7), channel_id=1, replica_groups=mesh['gz'=8,'gy'=4] {'gz','gy'}, dimensions={0} | all-to-all | bytes 1835008 | tf_op jit(solution)/shard_map/all_to_all | solution.py:626
  54.7 4.1 %unpack.1 = f32[16,32,2048]{2,1,0:T(8,128)} custom-call(f32[1792,128]{1,0:T(8,128)S(1)} %bitcast.5, bf16[256,256]{1,0:T(8,128)(2,1)S(1)} %get-tuple-element.20.real_table, bf16[768,512]{1,0:T(8,128)(2,1)S(1)} %get-tuple-element.21.full_table, bf16[512,256]{1,0:T(8,128)(2,1)S(1)} %get-tuple-element.22.stencil), custom_call_target="tpu_custom_call" | custom-call | tf_op jit(solution)/shard_map/unpack/pallas_call | solution.py:680

commit v2 on v1

--- a/solution.py
+++ b/solution.py
@@ -65,11 +65,11 @@
     return np.kron(small, np.eye(replicas))
 
 
-def slot_rows(plan, modes, at):
+def slot_rows(plan, modes, at, shared=True):
     made = []
     for mode in modes:
         angle = 2.0 * np.pi * mode * at / plan.count
-        if mode == 0:
+        if shared and mode == 0:
             made.append(np.concatenate([np.cos(angle), np.sin(angle)]))
             flip = np.pi * at
             made.append(np.concatenate([np.cos(flip), np.sin(flip)]))
@@ -79,36 +79,51 @@
     return np.stack(made)
 
 
+def shared_slot(plan, table):
+    half = plan.replicas // 2
+    order = [
+        (j // half) * plan.replicas + j % half + half * c
+        for c in range(2)
+        for j in range(plan.replicas)
+    ]
+    return np.concatenate([table[order], table[plan.block :]])
+
+
+def full_rows(plan):
+    modes = range(0, plan.count, plan.radix)
+    return slot_rows(plan, modes, np.arange(plan.fine_x), shared=False)
+
+
 def pack_tables(plan):
     at = np.arange(plan.fine_x)
-    real, full = [], []
-    for first, modes in plan.groups:
-        small = slot_rows(plan, modes, at)
-        if first in (0, plan.radix // 2):
-            real.append(side_by_side(spread(small[:, : plan.fine_x], plan.replicas)))
-        else:
-            full.append(side_by_side(spread(small, plan.replicas)))
+    real = []
+    for first, modes in plan.groups[:2]:
+        table = spread(slot_rows(plan, modes, at)[:, : plan.fine_x], plan.replicas)
+        real.append(side_by_side(shared_slot(plan, table) if first == 0 else table))
+    turns = np.zeros((2 * plan.radix, LANES))
+    for first in range(plan.radix):
+        angle = np.repeat(2.0 * np.pi * first * at / plan.count, plan.replicas)
+        turns[first], turns[plan.radix + first] = np.cos(angle), -np.sin(angle)
     modes = [mode for _, group in plan.groups for mode in group]
     every = slot_rows(plan, modes, np.arange(plan.count))[:, : plan.count]
     every = np.concatenate([every[0::2], every[1::2]])
-    return np.concatenate(real), np.concatenate(full), every.astype(np.float32)
+    full = side_by_side(spread(full_rows(plan), plan.replicas))
+    single = np.float32
+    return np.concatenate(real), full, every.astype(single), turns.astype(single)
 
 
 def unpack_tables(plan):
     at = np.arange(plan.fine_x)
-    real, full = [], []
-    for first, modes in plan.groups:
-        rows = slot_rows(plan, modes, at)
-        re_of, im_of = rows[:, : plan.fine_x].T, rows[:, plan.fine_x :].T
-        if first in (0, plan.radix // 2):
-            weight = np.full(re_of.shape, 2.0 / plan.count)
-            if first == 0:
-                weight[:, :2] = 1.0 / plan.count
-            real.append(side_by_side(spread(re_of * weight, plan.replicas)))
-        else:
-            both = np.concatenate([re_of, im_of]) / plan.count
-            full.append(side_by_side(spread(both, plan.replicas)))
-    return np.concatenate(real), np.concatenate(full)
+    real = []
+    for first, modes in plan.groups[:2]:
+        re_of = slot_rows(plan, modes, at)[:, : plan.fine_x].T
+        weight = np.full(re_of.shape, 2.0 / plan.count)
+        if first == 0:
+            weight[:, :2] = 1.0 / plan.count
+        table = spread(re_of * weight, plan.replicas)
+        real.append(side_by_side(shared_slot(plan, table.T).T if first == 0 else table))
+    full = side_by_side(spread(full_rows(plan).T / plan.count, plan.replicas))
+    return np.concatenate(real), full
 
 
 def plane_tables(plan):
@@ -122,58 +137,42 @@
     angle = 2 * np.pi * (np.outer(z_at, z_at) / plan.planes + np.outer(y_at, y_at) / plan.rows)
     cosine, sine = np.cos(angle), np.sin(angle)
     there = np.block([[cosine, -sine], [sine, cosine]])
-    scale = 1.0 / (count * count)
-    again = np.block([[cosine, sine], [-sine, cosine]]) * scale
     angle = 2 * np.pi * (np.outer(z_of, z_of) / plan.nz + np.outer(y_of, y_of) / plan.ny)
     cosine, sine = np.cos(angle), np.sin(angle)
     blocks = np.block([[cosine, sine], [-sine, cosine], [cosine, -sine], [-sine, -cosine]])
-    return twist, blocks.astype(np.float32), side_by_side(there), side_by_side(again)
-
-
-def halo_moves(plan):
+    return twist, blocks.astype(np.float32), side_by_side(there), side_table(plan)
+
+
+def halo_places(plan):
     planes, rows = plan.planes, plan.rows
     quarter = LANES // 4
-    taken = {0, 1, planes - 1}
-    open_groups = [
-        g for g in range(planes)
-        if g not in taken and not 2 * quarter <= g * rows < 3 * quarter
+    open_lanes = [
+        lane
+        for lane in range(2 * rows, (planes - 1) * rows)
+        if not 2 * quarter <= lane < 3 * quarter
     ]
-    used = {g: 0 for g in open_groups}
-    moves, where = [], {}
-    for source, left in (("own", set(range(planes))), ("corner", {planes - 1, 0, 1})):
-        while left:
-            best = None
-            for shift in range(planes):
-                for slot in range(rows // 3):
-                    hits = [
-                        z for z in left
-                        if (z + shift) % planes in used and used[(z + shift) % planes] == slot
-                    ]
-                    if best is None or len(hits) > len(best[2]):
-                        best = (shift, slot, hits)
-            shift, slot, hits = best
-            lanes = []
-            for z in hits:
-                group = (z + shift) % planes
-                used[group] += 1
-                left.discard(z)
-                plane = z
-                if source == "corner":
-                    plane = -1 if z == planes - 1 else planes + z
-                for step, row in enumerate((rows, rows + 1, -1)):
-                    lane = group * rows + 3 * slot + step
-                    lanes.append(lane)
-                    where[(plane, row)] = lane
-            moves.append((source, (shift * rows + 3 * slot) % LANES, tuple(sorted(lanes))))
+    sides = [(z, y) for z in range(-1, planes + 2) for y in (-1, rows, rows + 1)]
+    places = dict(zip(sides, open_lanes, strict=False))
     for row in range(rows):
-        where[(-1, row)] = (planes - 1) * rows + row
-        where[(planes, row)] = row
-        where[(planes + 1, row)] = rows + row
-    return moves, where
+        places[(-1, row)] = (planes - 1) * rows + row
+        places[(planes, row)] = row
+        places[(planes + 1, row)] = rows + row
+    return places
+
+
+def side_table(plan):
+    planes, rows = plan.planes, plan.rows
+    table = np.zeros((2 * LANES, LANES))
+    for (z, y), lane in halo_places(plan).items():
+        if 0 <= y < rows:
+            continue
+        source = z % planes * rows + y % rows
+        table[source if 0 <= z < planes else LANES + source, lane] = 1.0
+    return table.astype(jnp.bfloat16)
 
 
 def stencil_table(plan):
-    _, where = halo_moves(plan)
+    where = halo_places(plan)
 
     def line(size):
         made = np.zeros((2 * size, size + 3))
@@ -183,8 +182,8 @@
                 made[2 * i + 1, i + 1 + step] = weight
         return made
 
-    along_z, along_y = line(plan.planes), line(plan.rows)
-    table = np.zeros((4 * plan.planes * plan.rows, 2 * LANES))
+    along_z, along_y = np.eye(plan.planes + 3), line(plan.rows)
+    table = np.zeros((2 * (plan.planes + 3) * plan.rows, 2 * LANES))
     for z in range(-1, plan.planes + 2):
         for y in range(-1, plan.rows + 2):
             if 0 <= z < plan.planes and 0 <= y < plan.rows:
@@ -316,12 +315,12 @@
 
 
 def pack_kernel(plan, ahead, _, *refs):
-    sources, later = refs[:5], refs[5 : 5 + ahead]
-    out, carried = refs[5 + ahead], refs[6 + ahead : 6 + 2 * ahead]
-    targets, arrivals, others = refs[-7:-2], refs[-2], refs[-1]
+    sources, later = refs[:6], refs[6 : 6 + ahead]
+    out, carried = refs[6 + ahead], refs[7 + ahead : 7 + 2 * ahead]
+    targets, arrivals, others = refs[-8:-2], refs[-2], refs[-1]
     copies = fetches(sources, targets, arrivals)
     later_copies = fetches(later, carried, others)
-    charges, kernel, real_table, full_table, kernel_table = targets
+    charges, kernel, real_table, full_table, kernel_table, turns = targets
     width, block = LANES, plan.block
     copies[0].wait()
     tiles = [
@@ -330,7 +329,7 @@
     ]
     spectrum = from_real(tiles)
     copies[2].wait()
-    slot, real_at, full_at = 0, 0, 0
+    slot, real_at = 0, 0
     for first, modes in plan.groups:
         re, im = spectrum[first]
         size = len(modes) * block
@@ -339,10 +338,12 @@
             real_at += size
             values = re
         else:
-            if full_at == 0:
+            if first == 1:
                 copies[3].wait()
-            columns, table, at = 2 * width, full_table, full_at
-            full_at += size
+                copies[5].wait()
+            columns, table, at = 2 * width, full_table, 0
+            c, s = turns[first : first + 1, :], turns[plan.radix + first : plan.radix + first + 1, :]
+            re, im = re * c - im * s, re * s + im * c
             values = jnp.concatenate([re, im], axis=1)
         high, low = split(values)
         w_high = table[at : at + size, :columns]
@@ -366,21 +367,18 @@
         copy.wait()
 
 
-def plane_kernel(plan, ahead, shared, arrived, *refs):
-    twist, blocks, there, again = refs[:4]
-    later, out, carried = refs[4 : 4 + ahead], refs[4 + ahead], refs[5 + ahead : 5 + 2 * ahead]
-    first_pass, spectra, gains, high_part, low_part, others = refs[-6:]
-    later_copies = fetches(later, carried, others)
+def plane_kernel(plan, shared, arrived, *refs):
+    twist, blocks, there, sides, out = refs[:5]
+    first_pass, spectra, gains, high_part, low_part, edges = refs[5:]
     nz, ny, parts, reps = plan.nz, plan.ny, plan.parts, plan.replicas
     whole = 2 * LANES
 
-    def both(table):
-        high, low = table[:, :whole], table[:, whole:]
-        return jnp.concatenate([high, high, low], axis=0)
-
-    def apply(table, size):
+    def apply(size, back):
         high, low = high_part[:size, :], low_part[:size, :]
-        return dot(jnp.concatenate([high, low, high], axis=1), both(table), NN)
+        values = jnp.concatenate([high, low, high], axis=1)
+        high, low = there[:, :whole], there[:, whole:]
+        table = jnp.concatenate([high, high, low], axis=1 if back else 0)
+        return dot(values, table, NT if back else NN)
 
     def twisted(re, im, t, sign):
         c = twist[t : t + 1, :]
@@ -410,17 +408,17 @@
         re = lines[2 * k * parts : (2 * k + 1) * parts]
         im = lines[(2 * k + 1) * parts : (2 * k + 2) * parts]
         put(k * parts, parts, re * c - im * s, re * s + im * c)
-    made = apply(there, 2 * parts)
+    made = apply(2 * parts, False)
     plus_re, plus_im = made[:parts, :LANES], made[:parts, LANES:]
     minus_re, minus_im = made[parts:, :LANES], made[parts:, LANES:]
     a_re, a_im = 0.5 * (plus_re + minus_re), 0.5 * (plus_im + minus_im)
     b_re, b_im = 0.5 * (plus_im - minus_im), 0.5 * (minus_re - plus_re)
     is_shared = shared[0] == 0
-    zero = jnp.zeros_like(a_re)
-    gains[0 * parts : 1 * parts, :] = jnp.where(is_shared, 0.5 * (a_re + b_re), plus_re)
-    gains[1 * parts : 2 * parts, :] = jnp.where(is_shared, 0.5 * (a_im + b_im), plus_im)
-    gains[2 * parts : 3 * parts, :] = jnp.where(is_shared, 0.5 * (a_re - b_re), zero)
-    gains[3 * parts : 4 * parts, :] = jnp.where(is_shared, 0.5 * (a_im - b_im), zero)
+    scale = 1.0 / (plan.count * plan.count)
+    for k, (own, mixed) in enumerate(
+        ((plus_re, a_re), (plus_im, a_im), (plus_re, b_re), (plus_im, b_im))
+    ):
+        gains[k * parts : (k + 1) * parts, :] = jnp.where(is_shared, mixed, own) * scale
 
     for kz in range(nz):
         values = []
@@ -430,21 +428,18 @@
         for ky, (re, im) in enumerate(transform(values, -1)):
             t = kz * ny + ky
             put(t * reps, reps, *twisted(re, im, t, 1.0))
-            mirror = (-kz % nz) * ny + (-ky % ny)
-            put((parts + mirror) * reps, reps, *twisted(re, -im, mirror, 1.0))
-    spectra[...] = apply(there, 2 * parts * reps)
+    spectra[...] = apply(parts * reps, False)
 
     for t in range(parts):
-        u_re, u_im = gains[t : t + 1, :], gains[parts + t : parts + t + 1, :]
-        v_re = gains[2 * parts + t : 2 * parts + t + 1, :]
-        v_im = gains[3 * parts + t : 3 * parts + t + 1, :]
-        at, other = t * reps, (parts + t) * reps
-        s_re, s_im = spectra[at : at + reps, :LANES], spectra[at : at + reps, LANES:]
-        m_re, m_im = spectra[other : other + reps, :LANES], spectra[other : other + reps, LANES:]
-        re = (u_re * s_re - u_im * s_im) + (v_re * m_re - v_im * m_im)
-        im = (u_re * s_im + u_im * s_re) + (v_re * m_im + v_im * m_re)
-        put(at, reps, re, im)
-    spectra[: parts * reps, :] = apply(again, parts * reps)
+        made = []
+        for piece in range(2):
+            at = t * reps + piece * SUBLANES
+            k = 2 * piece * parts + t
+            u_re, u_im = gains[k : k + 1, :], gains[parts + k : parts + k + 1, :]
+            s_re, s_im = spectra[at : at + SUBLANES, :LANES], spectra[at : at + SUBLANES, LANES:]
+            made.append((u_re * s_re - u_im * s_im, u_re * s_im + u_im * s_re))
+        put(t * reps, reps, *(jnp.concatenate(pair, axis=0) for pair in zip(*made)))
+    spectra[...] = apply(parts * reps, True)
 
     for kz in range(nz):
         values = []
@@ -467,157 +462,151 @@
             out[at : at + reps, :] = re
             out[at + reps : at + 2 * reps, :] = im
 
-    moves, _ = halo_moves(plan)
-    rows, planes = plan.rows, plan.planes
-    lane = lax.broadcasted_iota(jnp.int32, (SUBLANES, LANES), 1)
-    comb = lane % rows
-
-    def among(lanes):
-        mask = lane < 0
-        start = None
-        for l in list(lanes) + [None]:
-            if start is None:
-                start, last = l, l
-            elif l == last + 1 if l is not None else False:
-                last = l
-            else:
-                mask = mask | ((lane >= start) & (lane <= last))
-                start, last = l, l
-        return mask
-
-    masks = [among(lanes) for _, _, lanes in moves]
-    before_mask = comb == 2
-    last_plane = lane >= (planes - 1) * rows
+    block, rows = plan.block, plan.rows
+    lane = lax.broadcasted_iota(jnp.int32, (block, LANES), 1)
+    quarter = LANES // 4
+    before = lane % rows == rows - 1
+    last_plane = lane >= (plan.planes - 1) * rows
     first_planes = lane < 2 * rows
-    quarter = LANES // 4
     spare = (lane >= 2 * quarter) & (lane < 3 * quarter)
-    pieces = plan.block // SUBLANES
-
-    def main(gz, gy, piece):
-        at = ((gz % nz) * ny + gy % ny) * plan.back + piece * SUBLANES
-        return out[at : at + SUBLANES, :]
-
-    def roll(values, shift):
-        shift %= LANES
-        return values if shift == 0 else pltpu.roll(values, shift, 1)
-
-    for gy in range(ny):
-        for piece in range(pieces):
-            combs = [
-                jnp.where(
-                    before_mask,
-                    roll(main(gz, gy - 1, piece), 3 - rows),
-                    main(gz, gy + 1, piece),
+
+    def main(gz, gy):
+        at = ((gz % nz) * ny + gy % ny) * plan.back
+        return out[at : at + block, :]
+
+    def beside(gz, gy):
+        at = ((gz % nz) * ny + gy % ny) * block
+        return slice(at, at + block)
+
+    for gz in range(nz):
+        for gy in range(ny):
+            side = jnp.where(before, main(gz, gy - 1), main(gz, gy + 1))
+            first_pass[beside(gz, gy), :] = side
+            high, low = split(side)
+            edges[beside(gz, gy), :LANES] = high
+            edges[beside(gz, gy), 2 * LANES : 3 * LANES] = low
+    for gz in range(nz):
+        for gy in range(ny):
+            corner = jnp.where(
+                last_plane, first_pass[beside(gz - 1, gy), :], first_pass[beside(gz + 1, gy), :]
+            )
+            high, low = split(corner)
+            edges[beside(gz, gy), LANES : 2 * LANES] = high
+            edges[beside(gz, gy), 3 * LANES :] = low
+    first_pass[...] = dot(edges[...], jnp.concatenate([sides[...], sides[...]], axis=0), NN)
+    for gz in range(nz):
+        for gy in range(ny):
+            made = jnp.where(first_planes, main(gz + 1, gy), first_pass[beside(gz, gy), :])
+            made = jnp.where(last_plane, main(gz - 1, gy), made)
+            extra = made[3 * SUBLANES :]
+            to = (gz * ny + gy) * plan.back + block
+            for piece, start in enumerate((0, quarter, 3 * quarter)):
+                value = made[piece * SUBLANES : (piece + 1) * SUBLANES]
+                moved = pltpu.roll(extra, (2 * quarter - start) % LANES, 1)
+                out[to + piece * SUBLANES : to + (piece + 1) * SUBLANES, :] = jnp.where(
+                    spare[:SUBLANES], moved, value
                 )
-                for gz in range(nz)
-            ]
-            for gz in range(nz):
-                corner = jnp.where(last_plane, combs[gz - 1], combs[(gz + 1) % nz])
-                made = None
-                for (source, shift, _), mask in zip(moves, masks):
-                    moved = roll(combs[gz] if source == "own" else corner, shift)
-                    made = moved if made is None else jnp.where(mask, moved, made)
-                made = jnp.where(first_planes, main(gz + 1, gy, piece), made)
-                made = jnp.where(last_plane, main(gz - 1, gy, piece), made)
-                at = ((gz * ny + gy) * pieces + piece) * SUBLANES
-                first_pass[at : at + SUBLANES, :] = made
-    for s in range(parts):
-        extra = first_pass[(s * pieces + pieces - 1) * SUBLANES : (s + 1) * pieces * SUBLANES, :]
-        for piece, start in enumerate((0, quarter, 3 * quarter)):
-            at = (s * pieces + piece) * SUBLANES
-            value = first_pass[at : at + SUBLANES, :]
-            to = s * plan.back + plan.block + piece * SUBLANES
-            out[to : to + SUBLANES, :] = jnp.where(spare, roll(extra, 2 * quarter - start), value)
-    for copy in later_copies:
-        copy.wait()
 
 
 def unpack_kernel(
-    plan, steps, arrived, real_table, full_table, stencil, out, inside, parts_of, coarse
+    plan, steps, arrived, real_table, full_table, stencil, out,
+    inside, parts_of, coarse, fine, sent,
 ):
     reps, block = plan.replicas, plan.block
     wide = 2 * LANES
-    step = pl.program_id(0)
-
-    @pl.when(step == 0)
-    def _():
-        lane = lax.broadcasted_iota(jnp.int32, (SUBLANES, LANES), 1)
-        quarter = LANES // 4
-        slot, real_at, full_at, part_at = 0, 0, 0, 0
-        found = {}
-        for first, modes in plan.groups:
-            for m in range(len(modes)):
-                at = (slot + m) * plan.back
-                inside[m * block : (m + 1) * block, :LANES] = arrived[at : at + block, :]
-                packed = [
-                    arrived[at + block + k * SUBLANES : at + block + (k + 1) * SUBLANES, :]
-                    for k in range(3)
-                ]
-                last = jnp.where(
-                    lane < quarter,
-                    pltpu.roll(packed[0], 2 * quarter, 1),
-                    jnp.where(
-                        lane < 2 * quarter,
-                        pltpu.roll(packed[1], 3 * quarter, 1),
-                        pltpu.roll(packed[2], quarter, 1),
-                    ),
-                )
-                for k, value in enumerate(packed + [last]):
-                    to = m * block + k * SUBLANES
-                    inside[to : to + SUBLANES, LANES:] = value
-            depth = len(modes) * block
-            high, low = split(inside[:depth, :])
-            both = jnp.concatenate([high, low, high], axis=0)
-            if first in (0, plan.radix // 2):
-                size, table, at = LANES, real_table, real_at
-                real_at += size
-            else:
-                size, table, at = 2 * LANES, full_table, full_at
-                full_at += size
-            w_high = table[at : at + size, :depth]
-            w_low = table[at : at + size, depth:]
-            made = dot(jnp.concatenate([w_high, w_high, w_low], axis=1), both, NN)
-            parts_of[part_at : part_at + size, :] = made
-            found[first] = (part_at, size > LANES)
-            part_at += size
-            slot += len(modes)
-        for x_l in range(plan.fine_x):
-            for piece in range(reps // SUBLANES):
-                row = x_l * reps + piece * SUBLANES
-                values = []
-                for first in range(plan.radix // 2 + 1):
-                    at, is_full = found[first]
-                    re = parts_of[at + row : at + row + SUBLANES, :]
-                    im = None
-                    if is_full:
-                        im = parts_of[at + LANES + row : at + LANES + row + SUBLANES, :]
-                    values.append((re, im))
-                for xh, value in enumerate(to_real(values)):
-                    x = xh * plan.fine_x + x_l
-                    places = [x + 1]
-                    if x == plan.count - 1:
-                        places.append(0)
-                    if x < 2:
-                        places.append(x + 1 + plan.count)
-                    for place in places:
-                        to = place * reps + piece * SUBLANES
-                        coarse[to : to + SUBLANES, :] = value
+    lane = lax.broadcasted_iota(jnp.int32, (SUBLANES, LANES), 1)
+    quarter = LANES // 4
+    slot, real_at, part_at = 0, 0, 0
+    found = {}
+    for first, modes in plan.groups:
+        for m in range(len(modes)):
+            at = (slot + m) * plan.back
+            inside[m * block : (m + 1) * block, :LANES] = arrived[at : at + block, :]
+            packed = [
+                arrived[at + block + k * SUBLANES : at + block + (k + 1) * SUBLANES, :]
+                for k in range(3)
+            ]
+            last = jnp.where(
+                lane < quarter,
+                pltpu.roll(packed[0], 2 * quarter, 1),
+                jnp.where(
+                    lane < 2 * quarter,
+                    pltpu.roll(packed[1], 3 * quarter, 1),
+                    pltpu.roll(packed[2], quarter, 1),
+                ),
+            )
+            for k, value in enumerate(packed + [last]):
+                to = m * block + k * SUBLANES
+                inside[to : to + SUBLANES, LANES:] = value
+        depth = len(modes) * block
+        high, low = split(inside[:depth, :])
+        both = jnp.concatenate([high, low, high], axis=0)
+        if first in (0, plan.radix // 2):
+            size, table, at = LANES, real_table, real_at
+            real_at += size
+        else:
+            size, table, at = 2 * LANES, full_table, 0
+        w_high = table[at : at + size, :depth]
+        w_low = table[at : at + size, depth:]
+        made = dot(jnp.concatenate([w_high, w_high, w_low], axis=1), both, NN)
+        parts_of[part_at : part_at + size, :] = made
+        found[first] = (part_at, size > LANES)
+        part_at += size
+        slot += len(modes)
+    for x_l in range(plan.fine_x):
+        for piece in range(reps // SUBLANES):
+            row = x_l * reps + piece * SUBLANES
+            values = []
+            for first in range(plan.radix // 2 + 1):
+                at, is_full = found[first]
+                re = parts_of[at + row : at + row + SUBLANES, :]
+                im = None
+                if is_full:
+                    im = parts_of[at + LANES + row : at + LANES + row + SUBLANES, :]
+                value = (re, im)
+                if is_full:
+                    value = turn(value, 2.0 * math.pi * first * x_l / plan.count)
+                values.append(value)
+            for xh, value in enumerate(to_real(values)):
+                x = xh * plan.fine_x + x_l
+                places = [x + 1]
+                if x == plan.count - 1:
+                    places.append(0)
+                if x < 2:
+                    places.append(x + 1 + plan.count)
+                for place in places:
+                    to = place * reps + piece * SUBLANES
+                    coarse[to : to + SUBLANES, :] = value
 
     here = plan.count // steps
-    made = []
-    for i in range(here):
-        taps = []
-        for move in range(4):
-            at = pl.multiple_of((step * here + i + move) * reps, reps)
-            taps.append(coarse[pl.ds(at, reps), :])
-        made.append(taps[1])
-        made.append((taps[1] + taps[2]) * (9.0 / 16.0) - (taps[0] + taps[3]) * (1.0 / 16.0))
-    high, low = split(jnp.concatenate(made, axis=0))
-    table = stencil[...]
-    fine = dot(
-        jnp.concatenate([table, table], axis=1), jnp.concatenate([high, low], axis=1), NT
-    )
-    out[...] = fine.reshape(out.shape)
+    table = jnp.concatenate([stencil[...], stencil[...]], axis=1)
+    width = out.shape[2] // steps
+    copies = []
+    for step in range(steps):
+        made = []
+        for i in range(here):
+            taps = []
+            for move in range(4):
+                at = (step * here + i + move) * reps
+                taps.append(coarse[at : at + reps, :])
+            made.append(taps[1])
+            made.append((taps[1] + taps[2]) * (9.0 / 16.0) - (taps[0] + taps[3]) * (1.0 / 16.0))
+        high, low = split(jnp.concatenate(made, axis=0))
+        values = dot(table, jnp.concatenate([high, low], axis=1), NT)
+        values = values.reshape(plan.planes + 3, 2 * plan.rows, width)
+        for z in range(plan.planes):
+            fine[step, 2 * z] = values[z + 1]
+            fine[step, 2 * z + 1] = (values[z + 1] + values[z + 2]) * (9.0 / 16.0) - (
+                values[z] + values[z + 3]
+            ) * (1.0 / 16.0)
+        copies.append(
+            pltpu.make_async_copy(
+                fine.at[step], out.at[:, :, step * width : (step + 1) * width], sent.at[step]
+            )
+        )
+        copies[-1].start()
+    for copy in copies:
+        copy.wait()
 
 
 def exchanged(values, parts):
@@ -655,42 +644,41 @@
     packed = exchanged(packed, parts)
 
     later = [jnp.asarray(t) for t in unpack_tables(plan) + (stencil_table(plan),)]
-    planes, *later = pl.pallas_call(
-        functools.partial(plane_kernel, plan, len(later)),
-        out_shape=[jax.ShapeDtypeStruct((parts * plan.back, LANES), f32)] + like(later),
-        in_specs=[SMEM] + [VMEM] * (1 + len(tables)) + [HBM] * len(later),
-        out_specs=[VMEM] * (1 + len(later)),
+    planes = pl.pallas_call(
+        functools.partial(plane_kernel, plan),
+        out_shape=jax.ShapeDtypeStruct((parts * plan.back, LANES), f32),
+        in_specs=[SMEM] + [VMEM] * (1 + len(tables)),
+        out_specs=VMEM,
         scratch_shapes=[
             pltpu.VMEM((parts * block, LANES), f32),
-            pltpu.VMEM((2 * parts * reps, 2 * LANES), f32),
+            pltpu.VMEM((parts * reps, 2 * LANES), f32),
             pltpu.VMEM((4 * parts, LANES), f32),
-            pltpu.VMEM((2 * parts * reps, 2 * LANES), bf16),
-            pltpu.VMEM((2 * parts * reps, 2 * LANES), bf16),
-            pltpu.SemaphoreType.DMA((len(later),)),
+            pltpu.VMEM((parts * reps, 2 * LANES), bf16),
+            pltpu.VMEM((parts * reps, 2 * LANES), bf16),
+            pltpu.VMEM((parts * block, 4 * LANES), bf16),
         ],
         compiler_params=limit,
         name="plane",
-    )(me, packed, *tables, *in_hbm(later))
+    )(me, packed, *tables)
     planes = exchanged(planes, parts)
 
-    steps = 4
+    steps = plan.radix
     fine_shape = (2 * plan.planes, 2 * plan.rows, 2 * plan.count * reps)
-    fixed = lambda shape: pl.BlockSpec(shape, lambda j: (0,) * len(shape))
-    operands = (planes, *later)
     return pl.pallas_call(
         functools.partial(unpack_kernel, plan, steps),
         out_shape=jax.ShapeDtypeStruct(fine_shape, f32),
-        grid=(steps,),
-        in_specs=[fixed(o.shape) for o in operands],
-        out_specs=pl.BlockSpec(fine_shape[:2] + (fine_shape[2] // steps,), lambda j: (0, 0, j)),
+        in_specs=[VMEM] * (1 + len(later)),
+        out_specs=HBM,
         scratch_shapes=[
             pltpu.VMEM((2 * LANES, 2 * LANES), f32),
             pltpu.VMEM((plan.radix * LANES, 2 * LANES), f32),
             pltpu.VMEM(((plan.count + 3) * reps, 2 * LANES), f32),
+            pltpu.VMEM((steps,) + fine_shape[:2] + (fine_shape[2] // steps,), f32),
+            pltpu.SemaphoreType.DMA((steps,)),
         ],
         compiler_params=limit,
         name="unpack",
-    )(*operands)
+    )(planes, *later)
 
 
 def extended(block, sides, width):

time: 59 us -> 57.3 us (0.971)
  Pallas kernels: 9.2 us -> 7.49 us
    pallas_call x1, Pallas kernels: 2.68 us -> 1.72 us  [fast_form(): pl.pallas_call(functools.partial(plane_kernel, plan), out_shape=jax.Shape...]
    pallas_call x1, Pallas kernels: 4.13 us -> 3.35 us  [fast_form(): pl.pallas_call(functools.partial(unpack_kernel, plan, steps), out_shape=j...]
where the time goes in v2:
time: 57.3 us; the launch traced here: 57.2 us
  blocking collectives  49.6 us (87%)
  Pallas kernels  7.49 us (13%)
    all_to_all x2, blocking collectives, exchanged(): lax.all_to_all(values, ('gz', 'gy'), split_axis=0, concat_axis=0, tiled=T...  49.6 us
    pallas_call x1, Pallas kernels, fast_form(): pl.pallas_call(functools.partial(unpack_kernel, plan, steps), out_shape=j...  3.35 us
    pallas_call x1, Pallas kernels, fast_form(): pl.pallas_call(functools.partial(pack_kernel, plan, len(tables)), out_sha...  2.41 us
    pallas_call x1, Pallas kernels, fast_form(): pl.pallas_call(functools.partial(plane_kernel, plan), out_shape=jax.Shape...  1.72 us

profile of v2, /device:TPU:0, one launch (start us, length us, event | category | flops | bytes accessed | tf_op | source)
XLA Modules:
  0.0 57.2 jit_solution(15808005524396499520)
XLA Ops:
  0.0 0.0 copy-start.1
  0.0 0.0 copy-start
  0.0 0.0 copy-start.2
  0.0 2.4 %pack.1 = (f32[1088,128]{1,0:T(8,128)S(1)}, f32[64,128]{1,0:T(8,128)S(1)}, f32[128,64]{1,0:T(8,128)S(1)}, bf16[256,512]{1,0:T(8,128)(2,1)S(1)}, bf16[256,128]{1,0:T(8,128)(2,1)S(1)}) custom-call(s32[1]{0:T(128)} %bitcast._.shared, f32[8,16,1024]{2,1,0:T(8,128)} %refs_0_.1, f32[8,16,64]{2,1,0:T(8,128)} %refs_1_.1, bf16[256,256]{1,0:T(8,128)(2,1)} %constant.33.clone.refs_2_, ...), custom_call_target="tpu_custom_call" | custom-call | tf_op jit(solution)/shard_map/pack/pallas_call | solution.py:635
  2.4 23.4 %all_to_all.10 = f32[32,1,4352]{2,1,0:T(1,128)S(1)} all-to-all(f32[32,1,4352]{2,1,0:T(1,128)S(1)} %bitcast.8), channel_id=1, replica_groups=mesh['gz'=8,'gy'=4] {'gz','gy'}, dimensions={0} | all-to-all | bytes 1114112 | tf_op jit(solution)/shard_map/all_to_all | solution.py:615
  25.8 1.7 %plane.1 = f32[1792,128]{1,0:T(8,128)S(1)} custom-call(s32[1]{0:T(128)} %bitcast._.shared, f32[1088,128]{1,0:T(8,128)S(1)} %bitcast.7, f32[64,128]{1,0:T(8,128)S(1)} %get-tuple-element.11.refs_0_, f32[128,64]{1,0:T(8,128)S(1)} %get-tuple-element.12.refs_1_, bf16[256,512]{1,0:T(8,128)(2,1)S(1)} %get-tuple-element.13.refs_2_, ...), custom_call_target="tpu_custom_call" | custom-call | tf_op jit(solution)/shard_map/plane/pallas_call | solution.py:647
  27.5 26.3 %all_to_all.11 = f32[32,1,7168]{2,1,0:T(1,128)S(1)} all-to-all(f32[32,1,7168]{2,1,0:T(1,128)S(1)} %bitcast.5), channel_id=1, replica_groups=mesh['gz'=8,'gy'=4] {'gz','gy'}, dimensions={0} | all-to-all | bytes 1835008 | tf_op jit(solution)/shard_map/all_to_all | solution.py:615
  53.8 0.0 copy-done.1
  53.8 0.0 copy-done
  53.8 0.0 copy-done.2
  53.8 3.4 %unpack.1 = f32[16,32,2048]{2,1,0:T(8,128)} custom-call(f32[1792,128]{1,0:T(8,128)S(1)} %bitcast.6, bf16[256,256]{1,0:T(8,128)(2,1)S(1)} %copy-done.2, bf16[256,512]{1,0:T(8,128)(2,1)S(1)} %copy-done, bf16[352,256]{1,0:T(8,128)(2,1)S(1)} %copy-done.1), custom_call_target="tpu_custom_call" | custom-call | tf_op jit(solution)/shard_map/unpack/pallas_call | solution.py:667
Async XLA Ops:
  0.0 53.8 %copy-start.1 = (bf16[352,256]{1,0:T(8,128)(2,1)S(1)}, bf16[352,256]{1,0:T(8,128)(2,1)}, u32[]{:S(2)}) copy-start(bf16[352,256]{1,0:T(8,128)(2,1)} %constant.43.clone.stencil) | copy-start | bytes 540676
  0.0 53.8 %copy-start = (bf16[256,512]{1,0:T(8,128)(2,1)S(1)}, bf16[256,512]{1,0:T(8,128)(2,1)}, u32[]{:S(2)}) copy-start(bf16[256,512]{1,0:T(8,128)(2,1)} %constant.42.clone.full_table) | copy-start | bytes 786436
  0.0 53.8 %copy-start.2 = (bf16[256,256]{1,0:T(8,128)(2,1)S(1)}, bf16[256,256]{1,0:T(8,128)(2,1)}, u32[]{:S(2)}) copy-start(bf16[256,256]{1,0:T(8,128)(2,1)} %constant.41.clone.real_table) | copy-start | bytes 393220

commit v3 on v2

--- a/solution.py
+++ b/solution.py
@@ -108,8 +108,10 @@
     every = slot_rows(plan, modes, np.arange(plan.count))[:, : plan.count]
     every = np.concatenate([every[0::2], every[1::2]])
     full = side_by_side(spread(full_rows(plan), plan.replicas))
-    single = np.float32
-    return np.concatenate(real), full, every.astype(single), turns.astype(single)
+    wide = np.zeros((plan.count, LANES))
+    wide[:, : plan.count] = every
+    singles = np.concatenate([turns, wide]).astype(np.float32)
+    return np.concatenate([full, np.concatenate(real, axis=1)]), singles
 
 
 def unpack_tables(plan):
@@ -140,7 +142,10 @@
     angle = 2 * np.pi * (np.outer(z_of, z_of) / plan.nz + np.outer(y_of, y_of) / plan.ny)
     cosine, sine = np.cos(angle), np.sin(angle)
     blocks = np.block([[cosine, sine], [-sine, cosine], [cosine, -sine], [-sine, -cosine]])
-    return twist, blocks.astype(np.float32), side_by_side(there), side_table(plan)
+    wide = np.zeros((blocks.shape[0], LANES), np.float32)
+    wide[:, : blocks.shape[1]] = blocks
+    doubles = np.concatenate([side_by_side(there), side_table(plan)], axis=1)
+    return np.concatenate([twist, wide]), doubles
 
 
 def halo_places(plan):
@@ -315,12 +320,12 @@
 
 
 def pack_kernel(plan, ahead, _, *refs):
-    sources, later = refs[:6], refs[6 : 6 + ahead]
-    out, carried = refs[6 + ahead], refs[7 + ahead : 7 + 2 * ahead]
-    targets, arrivals, others = refs[-8:-2], refs[-2], refs[-1]
+    sources, later = refs[:4], refs[4 : 4 + ahead]
+    out, carried = refs[4 + ahead], refs[5 + ahead : 5 + 2 * ahead]
+    targets, arrivals, others = refs[-6:-2], refs[-2], refs[-1]
     copies = fetches(sources, targets, arrivals)
     later_copies = fetches(later, carried, others)
-    charges, kernel, real_table, full_table, kernel_table, turns = targets
+    charges, kernel, table, singles = targets
     width, block = LANES, plan.block
     copies[0].wait()
     tiles = [
@@ -334,20 +339,20 @@
         re, im = spectrum[first]
         size = len(modes) * block
         if im is None:
-            columns, table, at = width, real_table, real_at
-            real_at += size
+            rows, at, columns = slice(2 * width, 3 * width), real_at, width
+            real_at += 2 * width
             values = re
         else:
             if first == 1:
                 copies[3].wait()
-                copies[5].wait()
-            columns, table, at = 2 * width, full_table, 0
-            c, s = turns[first : first + 1, :], turns[plan.radix + first : plan.radix + first + 1, :]
+            rows, at, columns = slice(0, 2 * width), 0, 2 * width
+            c = singles[first : first + 1, :]
+            s = singles[plan.radix + first : plan.radix + first + 1, :]
             re, im = re * c - im * s, re * s + im * c
             values = jnp.concatenate([re, im], axis=1)
         high, low = split(values)
-        w_high = table[at : at + size, :columns]
-        w_low = table[at : at + size, columns:]
+        w_high = table[rows, at : at + columns]
+        w_low = table[rows, at + columns : at + 2 * columns]
         made = dot(
             jnp.concatenate([w_high, w_high, w_low], axis=1),
             jnp.concatenate([high, low, high], axis=1),
@@ -358,8 +363,7 @@
             out[start : start + block, :] = made[m * block : (m + 1) * block]
         slot += len(modes)
     copies[1].wait()
-    copies[4].wait()
-    made = dot_exact(kernel_table[...], kernel[...].reshape(LANES, plan.count), NT)
+    made = dot_exact(singles[2 * plan.radix :, : plan.count], kernel[...].reshape(LANES, plan.count), NT)
     for c in range(2):
         rows = pl.ds(block + c, plan.parts, stride=plan.sent)
         out[rows, :] = made[c * plan.parts : (c + 1) * plan.parts]
@@ -368,15 +372,15 @@
 
 
 def plane_kernel(plan, shared, arrived, *refs):
-    twist, blocks, there, sides, out = refs[:5]
-    first_pass, spectra, gains, high_part, low_part, edges = refs[5:]
+    twist, there, out = refs[:3]
+    first_pass, spectra, gains, high_part, low_part, edges = refs[3:]
     nz, ny, parts, reps = plan.nz, plan.ny, plan.parts, plan.replicas
     whole = 2 * LANES
 
     def apply(size, back):
         high, low = high_part[:size, :], low_part[:size, :]
         values = jnp.concatenate([high, low, high], axis=1)
-        high, low = there[:, :whole], there[:, whole:]
+        high, low = there[:, :whole], there[:, whole : 2 * whole]
         table = jnp.concatenate([high, high, low], axis=1 if back else 0)
         return dot(values, table, NT if back else NN)
 
@@ -402,8 +406,8 @@
     lines = jnp.concatenate(
         [arrived[pl.ds(plan.block + c, parts, stride=plan.sent), :] for c in range(2)]
     )
-    lines = dot_exact(blocks[...], lines, NN)
-    c, s = twist[:parts, :], twist[parts:, :]
+    lines = dot_exact(twist[2 * parts :, : 2 * parts], lines, NN)
+    c, s = twist[:parts, :], twist[parts : 2 * parts, :]
     for k in range(2):
         re = lines[2 * k * parts : (2 * k + 1) * parts]
         im = lines[(2 * k + 1) * parts : (2 * k + 2) * parts]
@@ -493,7 +497,7 @@
             high, low = split(corner)
             edges[beside(gz, gy), LANES : 2 * LANES] = high
             edges[beside(gz, gy), 3 * LANES :] = low
-    first_pass[...] = dot(edges[...], jnp.concatenate([sides[...], sides[...]], axis=0), NN)
+    first_pass[...] = dot(edges[...], jnp.concatenate([there[:, 2 * whole :]] * 2, axis=0), NN)
     for gz in range(nz):
         for gy in range(ny):
             made = jnp.where(first_planes, main(gz + 1, gy), first_pass[beside(gz, gy), :])

time: 57.3 us -> 57.3 us (level)
  no operation moved by 1% of the time
where the time goes in v3:
time: 57.3 us; the launch traced here: 57.1 us
  blocking collectives  49.6 us (87%)
  Pallas kernels  7.48 us (13%)
    all_to_all x2, blocking collectives, exchanged(): lax.all_to_all(values, ('gz', 'gy'), split_axis=0, concat_axis=0, tiled=T...  49.6 us
    pallas_call x1, Pallas kernels, fast_form(): pl.pallas_call(functools.partial(unpack_kernel, plan, steps), out_shape=j...  3.36 us
    pallas_call x1, Pallas kernels, fast_form(): pl.pallas_call(functools.partial(pack_kernel, plan, len(tables)), out_sha...  2.4 us
    pallas_call x1, Pallas kernels, fast_form(): pl.pallas_call(functools.partial(plane_kernel, plan), out_shape=jax.Shape...  1.72 us

profile of v3, /device:TPU:0, one launch (start us, length us, event | category | flops | bytes accessed | tf_op | source)
XLA Modules:
  0.0 57.1 jit_solution(4996759805235052031)
XLA Ops:
  0.0 0.0 copy-start.1
  0.0 0.0 copy-start
  0.0 0.0 copy-start.2
  0.0 2.4 %pack.1 = (f32[1088,128]{1,0:T(8,128)S(1)}, f32[192,128]{1,0:T(8,128)S(1)}, bf16[256,640]{1,0:T(8,128)(2,1)S(1)}) custom-call(s32[1]{0:T(128)} %bitcast._.shared, f32[8,16,1024]{2,1,0:T(8,128)} %refs_0_.1, f32[8,16,64]{2,1,0:T(8,128)} %refs_1_.1, bf16[384,512]{1,0:T(8,128)(2,1)} %constant.25.clone.refs_2_, f32[80,128]{1,0:T(8,128)} %constant.26.clone.refs_3_, ...), custom_call_target="tpu_custom_call" | custom-call | tf_op jit(solution)/shard_map/pack/pallas_call | solution.py:639
  2.4 23.4 %all_to_all.10 = f32[32,1,4352]{2,1,0:T(1,128)S(1)} all-to-all(f32[32,1,4352]{2,1,0:T(1,128)S(1)} %bitcast.8), channel_id=1, replica_groups=mesh['gz'=8,'gy'=4] {'gz','gy'}, dimensions={0} | all-to-all | bytes 1114112 | tf_op jit(solution)/shard_map/all_to_all | solution.py:619
  25.8 1.7 %plane.1 = f32[1792,128]{1,0:T(8,128)S(1)} custom-call(s32[1]{0:T(128)} %bitcast._.shared, f32[1088,128]{1,0:T(8,128)S(1)} %bitcast.7, f32[192,128]{1,0:T(8,128)S(1)} %get-tuple-element.9.refs_0_, bf16[256,640]{1,0:T(8,128)(2,1)S(1)} %get-tuple-element.10.refs_1_), custom_call_target="tpu_custom_call" | custom-call | tf_op jit(solution)/shard_map/plane/pallas_call | solution.py:651
  27.5 26.3 %all_to_all.11 = f32[32,1,7168]{2,1,0:T(1,128)S(1)} all-to-all(f32[32,1,7168]{2,1,0:T(1,128)S(1)} %bitcast.5), channel_id=1, replica_groups=mesh['gz'=8,'gy'=4] {'gz','gy'}, dimensions={0} | all-to-all | bytes 1835008 | tf_op jit(solution)/shard_map/all_to_all | solution.py:619
  53.8 0.0 copy-done.1
  53.8 0.0 copy-done
  53.8 0.0 copy-done.2
  53.8 3.4 %unpack.1 = f32[16,32,2048]{2,1,0:T(8,128)} custom-call(f32[1792,128]{1,0:T(8,128)S(1)} %bitcast.6, bf16[256,256]{1,0:T(8,128)(2,1)S(1)} %copy-done.2, bf16[256,512]{1,0:T(8,128)(2,1)S(1)} %copy-done, bf16[352,256]{1,0:T(8,128)(2,1)S(1)} %copy-done.1), custom_call_target="tpu_custom_call" | custom-call | tf_op jit(solution)/shard_map/unpack/pallas_call | solution.py:671
Async XLA Ops:
  0.0 53.8 %copy-start.1 = (bf16[352,256]{1,0:T(8,128)(2,1)S(1)}, bf16[352,256]{1,0:T(8,128)(2,1)}, u32[]{:S(2)}) copy-start(bf16[352,256]{1,0:T(8,128)(2,1)} %constant.31.clone.stencil) | copy-start | bytes 540676
  0.0 53.8 %copy-start = (bf16[256,512]{1,0:T(8,128)(2,1)S(1)}, bf16[256,512]{1,0:T(8,128)(2,1)}, u32[]{:S(2)}) copy-start(bf16[256,512]{1,0:T(8,128)(2,1)} %constant.30.clone.full_table) | copy-start | bytes 786436
  0.0 53.8 %copy-start.2 = (bf16[256,256]{1,0:T(8,128)(2,1)S(1)}, bf16[256,256]{1,0:T(8,128)(2,1)}, u32[]{:S(2)}) copy-start(bf16[256,256]{1,0:T(8,128)(2,1)} %constant.29.clone.real_table) | copy-start | bytes 393220

commit v4 on v2

--- a/solution.py
+++ b/solution.py
@@ -604,7 +604,7 @@
                 fine.at[step], out.at[:, :, step * width : (step + 1) * width], sent.at[step]
             )
         )
-        copies[-1].start()
+        copies[-1].start(priority=step % 2)
     for copy in copies:
         copy.wait()
 

time: 57.3 us -> 57.3 us (level)
  no operation moved by 1% of the time
where the time goes in v4:
time: 57.3 us; the launch traced here: 57.2 us
  blocking collectives  49.6 us (87%)
  Pallas kernels  7.49 us (13%)
    all_to_all x2, blocking collectives, exchanged(): lax.all_to_all(values, ('gz', 'gy'), split_axis=0, concat_axis=0, tiled=T...  49.6 us
    pallas_call x1, Pallas kernels, fast_form(): pl.pallas_call(functools.partial(unpack_kernel, plan, steps), out_shape=j...  3.35 us
    pallas_call x1, Pallas kernels, fast_form(): pl.pallas_call(functools.partial(pack_kernel, plan, len(tables)), out_sha...  2.41 us
    pallas_call x1, Pallas kernels, fast_form(): pl.pallas_call(functools.partial(plane_kernel, plan), out_shape=jax.Shape...  1.72 us

profile of v4, /device:TPU:0, one launch (start us, length us, event | category | flops | bytes accessed | tf_op | source)
XLA Modules:
  0.0 57.2 jit_solution(16605005262903069838)
XLA Ops:
  0.0 0.0 copy-start.1
  0.0 0.0 copy-start
  0.0 0.0 copy-start.2
  0.0 2.4 %pack.1 = (f32[1088,128]{1,0:T(8,128)S(1)}, f32[64,128]{1,0:T(8,128)S(1)}, f32[128,64]{1,0:T(8,128)S(1)}, bf16[256,512]{1,0:T(8,128)(2,1)S(1)}, bf16[256,128]{1,0:T(8,128)(2,1)S(1)}) custom-call(s32[1]{0:T(128)} %bitcast._.shared, f32[8,16,1024]{2,1,0:T(8,128)} %refs_0_.1, f32[8,16,64]{2,1,0:T(8,128)} %refs_1_.1, bf16[256,256]{1,0:T(8,128)(2,1)} %constant.33.clone.refs_2_, ...), custom_call_target="tpu_custom_call" | custom-call | tf_op jit(solution)/shard_map/pack/pallas_call | solution.py:635
  2.4 23.4 %all_to_all.10 = f32[32,1,4352]{2,1,0:T(1,128)S(1)} all-to-all(f32[32,1,4352]{2,1,0:T(1,128)S(1)} %bitcast.8), channel_id=1, replica_groups=mesh['gz'=8,'gy'=4] {'gz','gy'}, dimensions={0} | all-to-all | bytes 1114112 | tf_op jit(solution)/shard_map/all_to_all | solution.py:615
  25.8 1.7 %plane.1 = f32[1792,128]{1,0:T(8,128)S(1)} custom-call(s32[1]{0:T(128)} %bitcast._.shared, f32[1088,128]{1,0:T(8,128)S(1)} %bitcast.7, f32[64,128]{1,0:T(8,128)S(1)} %get-tuple-element.11.refs_0_, f32[128,64]{1,0:T(8,128)S(1)} %get-tuple-element.12.refs_1_, bf16[256,512]{1,0:T(8,128)(2,1)S(1)} %get-tuple-element.13.refs_2_, ...), custom_call_target="tpu_custom_call" | custom-call | tf_op jit(solution)/shard_map/plane/pallas_call | solution.py:647
  27.5 26.3 %all_to_all.11 = f32[32,1,7168]{2,1,0:T(1,128)S(1)} all-to-all(f32[32,1,7168]{2,1,0:T(1,128)S(1)} %bitcast.5), channel_id=1, replica_groups=mesh['gz'=8,'gy'=4] {'gz','gy'}, dimensions={0} | all-to-all | bytes 1835008 | tf_op jit(solution)/shard_map/all_to_all | solution.py:615
  53.8 0.0 copy-done.1
  53.8 0.0 copy-done
  53.8 0.0 copy-done.2
  53.8 3.4 %unpack.1 = f32[16,32,2048]{2,1,0:T(8,128)} custom-call(f32[1792,128]{1,0:T(8,128)S(1)} %bitcast.6, bf16[256,256]{1,0:T(8,128)(2,1)S(1)} %copy-done.2, bf16[256,512]{1,0:T(8,128)(2,1)S(1)} %copy-done, bf16[352,256]{1,0:T(8,128)(2,1)S(1)} %copy-done.1), custom_call_target="tpu_custom_call" | custom-call | tf_op jit(solution)/shard_map/unpack/pallas_call | solution.py:667
Async XLA Ops:
  0.0 53.8 %copy-start.1 = (bf16[352,256]{1,0:T(8,128)(2,1)S(1)}, bf16[352,256]{1,0:T(8,128)(2,1)}, u32[]{:S(2)}) copy-start(bf16[352,256]{1,0:T(8,128)(2,1)} %constant.43.clone.stencil) | copy-start | bytes 540676
  0.0 53.8 %copy-start = (bf16[256,512]{1,0:T(8,128)(2,1)S(1)}, bf16[256,512]{1,0:T(8,128)(2,1)}, u32[]{:S(2)}) copy-start(bf16[256,512]{1,0:T(8,128)(2,1)} %constant.42.clone.full_table) | copy-start | bytes 786436
  0.0 53.8 %copy-start.2 = (bf16[256,256]{1,0:T(8,128)(2,1)S(1)}, bf16[256,256]{1,0:T(8,128)(2,1)}, u32[]{:S(2)}) copy-start(bf16[256,256]{1,0:T(8,128)(2,1)} %constant.41.clone.real_table) | copy-start | bytes 393220
